TPU v7x, 512 devices: a whole 4x8x8 slice. The times are simulated.
512 devices in a mesh: lat: 16 (over y, core), lon: 32 (over z, x).
Axes of the slice: x: 4, y: 8, z: 8, core: 2. Of those that a mesh axis runs over, the one named last changes fastest.
Arguments:
- forcing: float32 [2560, 4096], P('lat', 'lon'), may hold values from -28 to 28
- search_direction: float32 [2560, 4096], P('lat', 'lon'), may hold values from -28 to 28
- ocean_depth: float32 [2560, 4096], P('lat', 'lon'), may hold values from 0.5 to 8
- land_mask: int32 [2560, 4096], P('lat', 'lon'), may hold values 0 or 1
- fold_map: int32 [4096], replicated, may hold values from 0 to 4095, as said below
Outputs:
- scaled_height: float32 [2560, 4096], P('lat', 'lon')
- residual: float32 [2560, 4096], P('lat', 'lon')
Inputs may be any that keep to these rules, and one draw needn't show every extreme that they name: `fold_map`: column j's partner across the fold is (c - j) mod 4096 for one c of 0 to 4095, so the map is its own inverse.
All inputs are finite; a program needn't handle non-finite values. No bound on the sum of `land_mask` on one device may be relied on, other than what follows from the above.
Results may differ from a plain program's by a relative error of at most 0.0003.
Values sent between devices are 32-bit elements; how exact they have to be, the bound alone decides.
A program may use at most 64 MiB of HBM per device.

v0:
```python
import functools

import jax
import jax.numpy as jnp
from jax import lax
from jax.experimental import pallas as pl
from jax.experimental.pallas import tpu as pltpu
from jax.sharding import PartitionSpec as P

STEPS = 8
REACH = 256
LAT, LON, NX, NZ = 16, 32, 4, 8
ROWS, COLS = 160, 128
EXT = ROWS + 32
LO, HI = 8, 184
FIELDS = 2 * STEPS + 1
FIRST = STEPS + 1
HIGHEST = lax.Precision.HIGHEST
F32 = jnp.float32


def lanes_of(shape):
    return lax.broadcasted_iota(jnp.int32, shape, len(shape) - 1)


def from_east(main, side):
    lane = lanes_of(main.shape)
    a, b = pltpu.roll(main, COLS - 1, 1), pltpu.roll(side, COLS - 1, 1)
    last = lane == COLS - 1
    return jnp.where(last, b, a), jnp.where(last, a, b)


def from_west(main, side):
    lane = lanes_of(main.shape)
    a, b = pltpu.roll(main, 1, 1), pltpu.roll(side, 1, 1)
    head = lane == 0
    return jnp.where(head, b, a), jnp.where(head, a, b)


def remote(src, dst, send, recv, lat, lon):
    return pltpu.make_async_remote_copy(
        src_ref=src,
        dst_ref=dst,
        send_sem=send,
        recv_sem=recv,
        device_id={"lat": lat, "lon": lon},
        device_id_type=pl.DeviceIdType.MESH,
    )


CHUNK = 16


def far_first(count):
    return sorted(range(1, count), key=lambda d: (-min(d, count - d), d))


def chunks():
    return [(r, min(CHUNK, HI - r)) for r in range(LO, HI, CHUNK)]


def basis_kernel(
    fold_ref, forcing_ref, search_ref, depth_ref, mask_ref,
    basis_out, moments_out,
    raw_m, raw_h, depth_buf, mask_buf, pack_w, pack_e, got_w, got_e, corner,
    fold_x, fold_src, fold_z, fold_send, fold_got,
    wet_m, wet_h, s_m, s_h, de_m, de_h, se_m, se_h,
    w_m, w_h, b_m, b_h, rows_acc, part, red_x, red_z, red_y,
    local_sem, out_sem, halo_send, halo_recv, fz_send, fz_recv, fx_send, fx_recv,
    rx_send, rx_recv, rz_send, rz_recv, ry_send, ry_recv,
):
    lat = lax.axis_index("lat")
    lon = lax.axis_index("lon")
    zi, xi = lon // NX, lon % NX
    top = lat == LAT - 1
    bottom = lat == 0
    north, south = (lat + 1) % LAT, (lat + LAT - 1) % LAT
    east, west = (lon + 1) % LON, (lon + LON - 1) % LON
    barrier = pltpu.get_barrier_semaphore()

    peers = [(lat, ((zi + d) % NZ) * NX + xi) for d in far_first(NZ)]
    peers += [((lat + d) % LAT, lon) for d in far_first(LAT)]
    peers += [(north, east), (north, west), (south, east), (south, west)]
    peers += [(lat, zi * NX + (xi + d) % NX) for d in far_first(NX)]
    peers += [(lat, east), (lat, west)]
    for a, b in peers:
        pl.semaphore_signal(
            barrier, inc=1, device_id={"lat": a, "lon": b}, device_id_type=pl.DeviceIdType.MESH
        )

    loads = [
        pltpu.make_async_copy(depth_ref, depth_buf, local_sem.at[0]),
        pltpu.make_async_copy(mask_ref, mask_buf, local_sem.at[1]),
        pltpu.make_async_copy(forcing_ref, raw_m.at[1, pl.ds(16, ROWS), :], local_sem.at[2]),
        pltpu.make_async_copy(search_ref, raw_m.at[2, pl.ds(16, ROWS), :], local_sem.at[3]),
    ]
    for copy in loads:
        copy.start()
    rows_acc[...] = jnp.zeros_like(rows_acc)
    for copy in loads:
        copy.wait()
    raw_m[0, 16 : 16 + ROWS, :] = depth_buf[...] * mask_buf[...].astype(F32)

    lane40 = lanes_of((40, COLS))
    acc_w = jnp.zeros((40, COLS), F32)
    acc_e = jnp.zeros((40, COLS), F32)
    for g in range(4):
        for f in range(3):
            at = 32 * g + 9 * f
            block = raw_m[f, 16 + 40 * g : 56 + 40 * g, :]
            here = (lane40 >= at) & (lane40 < at + 9)
            acc_w = jnp.where(here, pltpu.roll(block, at, 1) if at else block, acc_w)
            acc_e = jnp.where(here, pltpu.roll(block, (at - 119) % COLS, 1), acc_e)
    pack_w[...] = acc_w
    pack_e[...] = acc_e

    pivot = fold_ref[0]
    pivot_block, pivot_lane = lax.shift_right_logical(pivot, 7), pivot & (COLS - 1)

    @pl.when(top)
    def _():
        fold_x[...] = jnp.zeros_like(fold_x)
        for m in range(9):
            fold_x[m : m + 1, :] = raw_m[0, 175 - m : 176 - m, :]
        for m in range(8):
            fold_x[9 + m : 10 + m, :] = raw_m[1, 175 - m : 176 - m, :]
            fold_x[17 + m : 18 + m, :] = raw_m[2, 175 - m : 176 - m, :]
        source = lax.broadcasted_iota(jnp.int32, (COLS, COLS), 0)
        target = lax.broadcasted_iota(jnp.int32, (COLS, COLS), 1)
        choose = (source == ((pivot - target) & (COLS - 1))).astype(F32)
        turned = jnp.dot(fold_x[...], choose, precision=HIGHEST, preferred_element_type=F32)
        fold_src[...] = turned
        fold_z[zi] = turned

    pl.semaphore_wait(barrier, len(peers))

    to_north = remote(raw_m.at[:, pl.ds(160, 16), :], raw_m.at[:, pl.ds(0, 16), :],
                      halo_send.at[0], halo_recv.at[0], north, lon)
    to_south = remote(raw_m.at[:, pl.ds(16, 16), :], raw_m.at[:, pl.ds(176, 16), :],
                      halo_send.at[1], halo_recv.at[1], south, lon)
    to_east = remote(pack_e, got_w, halo_send.at[2], halo_recv.at[2], lat, east)
    to_west = remote(pack_w, got_e, halo_send.at[3], halo_recv.at[3], lat, west)
    to_ne = remote(pack_e.at[pl.ds(24, 16), :], corner.at[0], halo_send.at[4], halo_recv.at[4], north, east)
    to_nw = remote(pack_w.at[pl.ds(24, 16), :], corner.at[1], halo_send.at[5], halo_recv.at[5], north, west)
    to_se = remote(pack_e.at[pl.ds(0, 16), :], corner.at[2], halo_send.at[6], halo_recv.at[6], south, east)
    to_sw = remote(pack_w.at[pl.ds(0, 16), :], corner.at[3], halo_send.at[7], halo_recv.at[7], south, west)

    fold_z_copies = []
    for d in range(1, NZ):
        peer = (zi + d) % NZ
        fold_z_copies.append(
            remote(fold_src, fold_z.at[zi], fz_send.at[d - 1], fz_recv.at[d - 1], lat, peer * NX + xi)
        )

    @pl.when(top)
    def _():
        for d in far_first(NZ):
            fold_z_copies[d - 1].start()

    @pl.when(jnp.logical_not(top))
    def _():
        to_ne.start()
        to_nw.start()
        to_north.start()

    @pl.when(jnp.logical_not(bottom))
    def _():
        to_se.start()
        to_sw.start()
        to_south.start()

    to_east.start()
    to_west.start()

    def fold_want(xt):
        want = (pivot_block - zi * NX - xt) & (LON - 1)
        return want

    @pl.when(top)
    def _():
        for d in range(1, NZ):
            fold_z_copies[d - 1].wait_recv()
        picks = []
        for d in range(NX):
            xt = (xi + d) % NX
            ahead = fold_want(xt) + 1
            block = ahead - ((ahead - xi) & (NX - 1))
            picks.append(fold_z[lax.shift_right_logical(block & (LON - 1), 2)])
        fold_got[xi] = picks[0]
        copies = []
        for d in range(1, NX):
            fold_send[d] = picks[d]
        for d in range(1, NX):
            copy = remote(fold_send.at[d], fold_got.at[xi], fx_send.at[d - 1], fx_recv.at[d - 1],
                          lat, zi * NX + (xi + d) % NX)
            copy.start()
            copies.append(copy)
        for copy in copies:
            copy.wait_recv()
        want = fold_want(xi)
        ahead2, here2, behind, behind2 = (
            fold_got[(want + 1) & 3], fold_got[want & 3], fold_got[(want - 1) & 3], fold_got[(want - 2) & 3]
        )
        lane = lanes_of((32, COLS))
        near = lane <= pivot_lane
        ghost_m = jnp.where(near, here2, behind)
        ghost_e = jnp.where(near, behind, behind2)
        ghost_w = jnp.where(near, ahead2, here2)
        ghost_h = jnp.where(lane < 9, ghost_e, jnp.where(lane >= 119, ghost_w, 0.0))
        for ref, ghost in ((raw_m, ghost_m), (raw_h, ghost_h)):
            for f in range(3):
                ref[f, 176:192, :] = jnp.zeros((16, COLS), F32)
            ref[0, 176:185, :] = ghost[0:9]
            ref[1, 176:184, :] = ghost[9:17]
            ref[2, 176:184, :] = ghost[17:25]
        for copy in copies:
            copy.wait_send()
        for copy in fold_z_copies:
            copy.wait_send()

    to_east.wait()
    to_west.wait()

    lane16 = lanes_of((16, COLS))
    for g in range(4):
        for f in range(3):
            at = 32 * g + 9 * f
            near_e = pltpu.roll(got_e[...], (COLS - at) % COLS, 1) if at else got_e[...]
            near_w = pltpu.roll(got_w[...], (119 - at) % COLS, 1)
            raw_h[f, 16 + 40 * g : 56 + 40 * g, :] = jnp.where(
                lane40 < 9, near_e, jnp.where(lane40 >= 119, near_w, 0.0)
            )

    @pl.when(jnp.logical_not(bottom))
    def _():
        to_se.wait_send()
        to_sw.wait_send()
        to_south.wait_send()
        to_ne.wait_recv()
        to_nw.wait_recv()
        to_north.wait_recv()
        for f in range(3):
            at = 96 + 9 * f
            near_e = pltpu.roll(corner[1], (COLS - at) % COLS, 1)
            near_w = pltpu.roll(corner[0], (119 - at) % COLS, 1)
            raw_h[f, 0:16, :] = jnp.where(lane16 < 9, near_e, jnp.where(lane16 >= 119, near_w, 0.0))

    @pl.when(bottom)
    def _():
        for f in range(3):
            raw_m[f, 0:16, :] = jnp.zeros((16, COLS), F32)
            raw_h[f, 0:16, :] = jnp.zeros((16, COLS), F32)

    @pl.when(jnp.logical_not(top))
    def _():
        to_ne.wait_send()
        to_nw.wait_send()
        to_north.wait_send()
        to_se.wait_recv()
        to_sw.wait_recv()
        to_south.wait_recv()
        for f in range(3):
            at = 9 * f
            near_e = pltpu.roll(corner[3], (COLS - at) % COLS, 1) if at else corner[3]
            near_w = pltpu.roll(corner[2], (119 - at) % COLS, 1)
            raw_h[f, 176:192, :] = jnp.where(lane16 < 9, near_e, jnp.where(lane16 >= 119, near_w, 0.0))

    for r, n in chunks():
        sums = []
        for raw in (raw_m, raw_h):
            up, mid, low = (raw[0, r + o : r + o + n, :] for o in (1, 0, -1))
            both = up + low
            wets = [(v > 0.0).astype(F32) for v in (up, mid, low)]
            both_wet = wets[0] + wets[2]
            sums.append((mid, both, mid + 0.5 * both, wets[1], both_wet, wets[1] + 0.5 * both_wet))
        (dm, bm, cm, wm, bwm, cwm), (dh, bh, ch, wh, bwh, cwh) = sums
        e_m, e_h = from_east(cm, ch)
        w_m_, w_h_ = from_west(cm, ch)
        ew_m, ew_h = from_east(cwm, cwh)
        ww_m, ww_h = from_west(cwm, cwh)
        rooted = []
        for depth, wet, all_depth, all_wet in (
            (dm, wm, bm + (e_m + w_m_), bwm + (ew_m + ww_m)),
            (dh, wh, bh + (e_h + w_h_), bwh + (ew_h + ww_h)),
        ):
            links = 0.5 * (depth * all_wet + all_depth)
            diagonal = wet * (depth * (1.0 / (REACH * REACH)) + links) + (1.0 - wet)
            rooted.append(wet * lax.rsqrt(diagonal))
        s_m[r : r + n, :], s_h[r : r + n, :] = rooted
        se_m[r : r + n, :], se_h[r : r + n, :] = from_east(*rooted)
        de_m[r : r + n, :], de_h[r : r + n, :] = from_east(dm, dh)
        b_m[0, r : r + n, :] = wm * raw_m[2, r : r + n, :]
        b_h[0, r : r + n, :] = wh * raw_h[2, r : r + n, :]
        b_m[FIRST, r : r + n, :] = wm * raw_m[1, r : r + n, :]
        b_h[FIRST, r : r + n, :] = wh * raw_h[1, r : r + n, :]

    for r, n in chunks():
        made = []
        for raw, s, de, se, w in ((raw_m, s_m, de_m, se_m, w_m), (raw_h, s_h, de_h, se_h, w_h)):
            d0, d1 = raw[0, r : r + n, :], raw[0, r + 1 : r + 1 + n, :]
            s0, s1 = s[r : r + n, :], s[r + 1 : r + 1 + n, :]
            de0, de1 = de[r : r + n, :], de[r + 1 : r + 1 + n, :]
            se0, se1 = se[r : r + n, :], se[r + 1 : r + 1 + n, :]
            east_w = -(d0 + de0) * (s0 * se0)
            ne_w = -0.5 * (d0 + de1) * (s0 * se1)
            nw_e = -0.5 * (de0 + d1) * (se0 * s1)
            w[0, r : r + n, :] = -(d0 + d1) * (s0 * s1)
            w[1, r : r + n, :] = east_w
            w[3, r : r + n, :] = ne_w
            w[6, r : r + n, :] = nw_e
            made.append((east_w, ne_w, nw_e))
        for slot, item in ((2, 0), (4, 1), (5, 2)):
            w_m[slot, r : r + n, :], w_h[slot, r : r + n, :] = from_west(made[0][item], made[1][item])

    def fold8(x):
        return sum(x[8 * k : 8 * k + 8] for k in range(x.shape[0] // 8))

    def row_slices(r, n):
        return max(r, 16) - r, min(r + n, 16 + ROWS) - r

    def step(n, both, first):
        bases = (0, FIRST) if both else (0,)
        total = [jnp.zeros((8, COLS), F32) for _ in range(6)]
        for r, size in chunks():
            weights = []
            for w in (w_m, w_h):
                weights.append((
                    w[0, r : r + size, :], w[0, r - 1 : r - 1 + size, :],
                    w[4, r : r + size, :], w[2, r : r + size, :], w[5, r - 1 : r - 1 + size, :],
                    w[6, r : r + size, :], w[1, r : r + size, :], w[3, r - 1 : r - 1 + size, :],
                ))
            news, olds = [], []
            for base in bases:
                zs = []
                for b, (a_u, a_d, e_u, e_c, e_d, f_u, f_c, f_d) in zip((b_m, b_h), weights):
                    k = base + n - 1
                    up = b[k, r + 1 : r + 1 + size, :]
                    mid = b[k, r : r + size, :]
                    low = b[k, r - 1 : r - 1 + size, :]
                    z0 = a_u * up + a_d * low
                    ze = e_u * up + e_c * mid + e_d * low
                    zw = f_u * up + f_c * mid + f_d * low
                    zs.append((mid, z0, ze, zw))
                (mid_m, z0_m, ze_m, zw_m), (mid_h, z0_h, ze_h, zw_h) = zs
                ze_m, ze_h = from_east(ze_m, ze_h)
                zw_m, zw_h = from_west(zw_m, zw_h)
                out_m, out_h = z0_m + (ze_m + zw_m), z0_h + (ze_h + zw_h)
                if first:
                    out_m, out_h = 0.5 * out_m, 0.5 * out_h
                else:
                    out_m = out_m - b_m[base + n - 2, r : r + size, :]
                    out_h = out_h - b_h[base + n - 2, r : r + size, :]
                b_m[base + n, r : r + size, :] = out_m
                b_h[base + n, r : r + size, :] = out_h
                news.append(out_m)
                olds.append(mid_m)
            lo, hi = row_slices(r, size)
            if hi > lo:
                p1, p0 = news[0][lo:hi], olds[0][lo:hi]
                total[0] = total[0] + fold8(p1 * p1)
                total[1] = total[1] + fold8(p1 * p0)
                if both:
                    r1, r0 = news[1][lo:hi], olds[1][lo:hi]
                    total[2] = total[2] + fold8(r1 * r1)
                    total[3] = total[3] + fold8(r1 * r0)
                    total[4] = total[4] + fold8(p1 * r1)
                else:
                    r0 = b_m[FIRST + STEPS - 1, r + lo : r + hi, :]
                total[5] = total[5] + fold8(p1 * r0)
        for c in range(6):
            rows_acc[pl.ds(6 * n + c, 1), :] = jnp.sum(total[c], axis=0, keepdims=True)

    start = [jnp.zeros((8, COLS), F32) for _ in range(3)]
    for r in range(16, 16 + ROWS, CHUNK):
        p0, r0 = b_m[0, r : r + CHUNK, :], b_m[FIRST, r : r + CHUNK, :]
        start = [t + fold8(v) for t, v in zip(start, (p0 * p0, r0 * r0, p0 * r0))]
    for c in range(3):
        rows_acc[2 * c : 2 * c + 1, :] = jnp.sum(start[c], axis=0, keepdims=True)

    step(1, True, True)

    @pl.loop(2, STEPS)
    def _(n):
        step(n, True, False)

    step(STEPS, False, False)

    outs = [
        pltpu.make_async_copy(b_m.at[k, pl.ds(16, ROWS), :], basis_out.at[k], out_sem.at[k])
        for k in range(FIELDS)
    ]
    for copy in outs:
        copy.start()

    ones = jnp.ones((8, COLS), F32)
    sums = lax.dot_general(
        ones, rows_acc[...], (((1,), (1,)), ((), ())), precision=HIGHEST, preferred_element_type=F32
    )[0:1]

    def reduce(stage, value, slots, send, recv, count, mine, peer_of, order):
        slots[mine] = value
        part[stage] = value
        copies = [
            remote(part.at[stage], slots.at[mine], send.at[d - 1], recv.at[d - 1], *peer_of(d))
            for d in range(1, count)
        ]
        for d in order:
            copies[d - 1].start()
        for copy in copies:
            copy.wait_recv()
        total = slots[0]
        for k in range(1, count):
            total = total + slots[k]
        return total, copies

    sums, first_copies = reduce(
        0, sums, red_x, rx_send, rx_recv, NX, xi,
        lambda d: (lat, zi * NX + (xi + d) % NX), far_first(NX))
    sums, second_copies = reduce(
        1, sums, red_z, rz_send, rz_recv, NZ, zi,
        lambda d: (lat, ((zi + d) % NZ) * NX + xi), far_first(NZ))
    sums, third_copies = reduce(
        2, sums, red_y, ry_send, ry_recv, LAT, lat,
        lambda d: ((lat + d) % LAT, lon), far_first(LAT))
    moments_out[...] = sums
    for copy in first_copies + second_copies + third_copies:
        copy.wait_send()
    for copy in outs:
        copy.wait()


def basis_and_moments(forcing, search, depth, mask, fold_map):
    vm = pltpu.VMEM
    dma = pltpu.SemaphoreType.DMA
    ext = (EXT, COLS)
    return pl.pallas_call(
        basis_kernel,
        grid=(1,),
        out_shape=(
            jax.ShapeDtypeStruct((FIELDS, ROWS, COLS), F32),
            jax.ShapeDtypeStruct((1, COLS), F32),
        ),
        in_specs=[pl.BlockSpec((1024,), lambda i: (0,), memory_space=pltpu.SMEM)]
        + [pl.BlockSpec(memory_space=pl.ANY)] * 4,
        out_specs=(
            pl.BlockSpec(memory_space=pl.ANY),
            pl.BlockSpec((1, COLS), lambda i: (0, 0)),
        ),
        scratch_shapes=[
            vm((3,) + ext, F32), vm((3,) + ext, F32),
            vm((ROWS, COLS), F32), vm((ROWS, COLS), jnp.int32),
            vm((40, COLS), F32), vm((40, COLS), F32), vm((40, COLS), F32), vm((40, COLS), F32),
            vm((4, 16, COLS), F32),
            vm((32, COLS), F32), vm((32, COLS), F32), vm((NZ, 32, COLS), F32),
            vm((NX, 32, COLS), F32), vm((NX, 32, COLS), F32),
        ]
        + [vm(ext, F32)] * 8
        + [vm((7,) + ext, F32)] * 2
        + [vm((FIELDS,) + ext, F32)] * 2
        + [
            vm((COLS, COLS), F32), vm((3, 1, COLS), F32),
            vm((NX, 1, COLS), F32), vm((NZ, 1, COLS), F32), vm((LAT, 1, COLS), F32),
            dma((4,)), dma((FIELDS,)), dma((8,)), dma((8,)),
            dma((NZ - 1,)), dma((NZ - 1,)), dma((NX - 1,)), dma((NX - 1,)),
            dma((NX - 1,)), dma((NX - 1,)), dma((NZ - 1,)), dma((NZ - 1,)),
            dma((LAT - 1,)), dma((LAT - 1,)),
        ],
        compiler_params=pltpu.CompilerParams(collective_id=0, has_side_effects=True),
        name="basis",
    )(fold_map, forcing, search, depth, mask)


def combine_kernel(moments_ref, basis_ref, height_ref, residual_ref):
    shape = (24, COLS)
    row = lax.broadcasted_iota(jnp.int32, shape, 0)
    col = lanes_of(shape)

    def power(i):
        return jnp.where(i >= FIRST, i - FIRST, i)

    kind = jnp.where((row >= FIRST) & (col >= FIRST), 1, jnp.where((row >= FIRST) | (col >= FIRST), 2, 0))
    valid = (row < FIELDS) & (col < FIELDS)
    ka, kb = power(row), power(col)
    high, low = ka + kb, jnp.abs(ka - kb)
    odd = high & 1

    def slot(k):
        return jnp.where(valid, 6 * ((k + 1) >> 1) + 2 * kind + odd, 0)

    base = jnp.where(odd == 1, 7 + 2 * kind, 2 * kind)
    raw = jnp.broadcast_to(moments_ref[...], shape)

    def take(index):
        return jnp.take_along_axis(raw, index, axis=1)

    gram = jnp.where(valid, take(slot(high)) + take(slot(low)) - take(jnp.where(valid, base, 0)), 0.0)

    def lower(i):
        return jnp.where((i == 1) | (i == FIRST + 1), 1.0, jnp.where((i >= 1) & (i < FIELDS) & (i != FIRST), 0.5, 0.0))

    def upper(i):
        return jnp.where((i < FIELDS - 2) & (i != FIRST - 2) & (i != FIRST - 1), 0.5, 0.0)

    low_l, up_l = lower(col).astype(F32), upper(col).astype(F32)
    low_s, up_s = lower(row).astype(F32), upper(row).astype(F32)

    def shifted(v, axis):
        length = v.shape[axis]
        low_c, up_c = (low_s, up_s) if axis == 0 else (low_l, up_l)
        return v + low_c * pltpu.roll(v, 1, axis) + up_c * pltpu.roll(v, length - 1, axis)

    below = pltpu.roll(low_l, COLS - 1, 1)
    above = pltpu.roll(up_l, 1, 1)
    ends = (col == FIRST - 1) | (col == FIELDS - 1)
    gram_h = jnp.where(
        ends, 0.0,
        gram + below * pltpu.roll(gram, COLS - 1, 1) + jnp.where(col > 0, above, 0.0) * pltpu.roll(gram, 1, 1),
    )

    def form(matrix, left, right):
        return jnp.sum(matrix * left * right, keepdims=True)

    unit = lambda at: ((row == at).astype(F32), (col == at).astype(F32))
    p_s, p_l = unit(0)
    r_s, r_l = unit(FIRST)
    q_s, q_l = shifted(p_s, 0), shifted(p_l, 1)
    x_s = jnp.zeros(shape, F32)
    norm = form(gram, r_s, r_l)
    curvature = form(gram_h, p_s, p_l)
    for inner in range(STEPS):
        t = norm / curvature
        x_s = x_s + t * p_s
        r_s = r_s - t * q_s
        if inner == STEPS - 1:
            break
        r_l = r_l - t * q_l
        h_s, h_l = shifted(r_s, 0), shifted(r_l, 1)
        fresh = form(gram, r_s, r_l)
        own = form(gram_h, r_s, r_l)
        cross = form(gram_h, r_s, p_l)
        beta = fresh / norm
        curvature = own + beta * (2.0 * cross + beta * curvature)
        norm = fresh
        p_s, p_l = r_s + beta * p_s, r_l + beta * p_l
        q_s, q_l = h_s + beta * q_s, h_l + beta * q_l

    size = 32
    for at in range(0, ROWS, size):
        height = jnp.zeros((size, COLS), F32)
        residual = jnp.zeros((size, COLS), F32)
        for k in range(FIELDS):
            field = basis_ref[k, at : at + size, :]
            height = height + x_s[k : k + 1, :] * field
            residual = residual + r_s[k : k + 1, :] * field
        height_ref[at : at + size, :] = height
        residual_ref[at : at + size, :] = residual


def per_device(forcing, search, depth, mask, fold_map):
    basis, moments = basis_and_moments(forcing, search, depth, mask, fold_map)
    block = jax.ShapeDtypeStruct((ROWS, COLS), F32)
    return pl.pallas_call(
        combine_kernel,
        out_shape=(block, block),
        name="combine",
    )(moments, basis)


def solution(mesh):
    return jax.shard_map(
        per_device,
        mesh=mesh,
        in_specs=(P("lat", "lon"),) * 4 + (P(),),
        out_specs=(P("lat", "lon"),) * 2,
        check_vma=False,
    )
```

profile of v0, /device:TPU:1, one launch (start us, length us, event | category | flops | bytes accessed | tf_op | source)
XLA Modules:
  0.0 43.2 jit_solution(9157146908761638633)
XLA Ops:
  0.6 39.1 %basis.1 = (f32[17,160,128]{2,1,0:T(8,128)}, f32[1,128]{1,0:T(1,128)}) custom-call(s32[4096]{0:T(1024)} %fold_ref.1, f32[160,128]{1,0:T(8,128)} %forcing_ref.1, f32[160,128]{1,0:T(8,128)} %search_ref.1, f32[160,128]{1,0:T(8,128)} %depth_ref.1, s32[160,128]{1,0:T(8,128)} %mask_ref.1), custom_call_target="tpu_custom_call" | custom-call | tf_op jit(solution)/shard_map/basis/pallas_call | solution.py:436
  39.7 3.4 %combine.1 = (f32[160,128]{1,0:T(8,128)}, f32[160,128]{1,0:T(8,128)}) custom-call(f32[1,128]{1,0:T(1,128)} %get-tuple-element.4.moments_ref, f32[17,160,128]{2,1,0:T(8,128)} %get-tuple-element.5.basis_ref), custom_call_target="tpu_custom_call" | custom-call | tf_op jit(solution)/shard_map/combine/pallas_call | solution.py:562
where the time goes:
time: 43.4 us; the launch traced here: 43.2 us
  Pallas kernels  42.5 us (98%)
  between operations  0.64 us (1%)
    pallas_call x1, Pallas kernels, basis_and_moments(): pl.pallas_call(basis_kernel, grid=(1,), out_shape=(jax.ShapeDtypeStruct((...  39.1 us
    pallas_call x1, Pallas kernels, per_device(): pl.pallas_call(combine_kernel, out_shape=(block, block), name='combine')  3.41 us

commit v1 on v0

--- a/solution.py
+++ b/solution.py
@@ -12,7 +12,7 @@
 LAT, LON, NX, NZ = 16, 32, 4, 8
 ROWS, COLS = 160, 128
 EXT = ROWS + 32
-LO, HI = 8, 184
+LO = 8
 FIELDS = 2 * STEPS + 1
 FIRST = STEPS + 1
 HIGHEST = lax.Precision.HIGHEST
@@ -55,19 +55,19 @@
     return sorted(range(1, count), key=lambda d: (-min(d, count - d), d))
 
 
-def chunks():
-    return [(r, min(CHUNK, HI - r)) for r in range(LO, HI, CHUNK)]
+def chunks(start, stop):
+    return [(r, min(CHUNK, stop - r)) for r in range(start, stop, CHUNK)]
 
 
 def basis_kernel(
     fold_ref, forcing_ref, search_ref, depth_ref, mask_ref,
-    basis_out, moments_out,
-    raw_m, raw_h, depth_buf, mask_buf, pack_w, pack_e, got_w, got_e, corner,
-    fold_x, fold_src, fold_z, fold_send, fold_got,
+    b_m, moments_out,
+    fold_buf, raw_m, raw_h, depth_buf, mask_buf, pack_w, pack_e, got_w, got_e, corner,
+    fold_x, fold_src, fold_row, fold_send, fold_got,
     wet_m, wet_h, s_m, s_h, de_m, de_h, se_m, se_h,
-    w_m, w_h, b_m, b_h, rows_acc, part, red_x, red_z, red_y,
-    local_sem, out_sem, halo_send, halo_recv, fz_send, fz_recv, fx_send, fx_recv,
-    rx_send, rx_recv, rz_send, rz_recv, ry_send, ry_recv,
+    w_m, w_h, b_h, rows_acc, part, red_p, red_y,
+    plane_sem, local_sem, halo_send, halo_recv, fz_send, fz_recv, fx_send, fx_recv,
+    rp_send, rp_recv, ry_send, ry_recv,
 ):
     lat = lax.axis_index("lat")
     lon = lax.axis_index("lon")
@@ -78,6 +78,15 @@
     east, west = (lon + 1) % LON, (lon + LON - 1) % LON
     barrier = pltpu.get_barrier_semaphore()
 
+    loads = [
+        pltpu.make_async_copy(depth_ref, depth_buf, local_sem.at[0]),
+        pltpu.make_async_copy(mask_ref, mask_buf, local_sem.at[1]),
+        pltpu.make_async_copy(forcing_ref, raw_m.at[1, pl.ds(16, ROWS), :], local_sem.at[2]),
+        pltpu.make_async_copy(search_ref, raw_m.at[2, pl.ds(16, ROWS), :], local_sem.at[3]),
+        pltpu.make_async_copy(fold_ref.at[pl.ds(0, 1024)], fold_buf, local_sem.at[4]),
+    ]
+    for copy in loads:
+        copy.start()
     peers = [(lat, ((zi + d) % NZ) * NX + xi) for d in far_first(NZ)]
     peers += [((lat + d) % LAT, lon) for d in far_first(LAT)]
     peers += [(north, east), (north, west), (south, east), (south, west)]
@@ -88,14 +97,6 @@
             barrier, inc=1, device_id={"lat": a, "lon": b}, device_id_type=pl.DeviceIdType.MESH
         )
 
-    loads = [
-        pltpu.make_async_copy(depth_ref, depth_buf, local_sem.at[0]),
-        pltpu.make_async_copy(mask_ref, mask_buf, local_sem.at[1]),
-        pltpu.make_async_copy(forcing_ref, raw_m.at[1, pl.ds(16, ROWS), :], local_sem.at[2]),
-        pltpu.make_async_copy(search_ref, raw_m.at[2, pl.ds(16, ROWS), :], local_sem.at[3]),
-    ]
-    for copy in loads:
-        copy.start()
     rows_acc[...] = jnp.zeros_like(rows_acc)
     for copy in loads:
         copy.wait()
@@ -114,7 +115,7 @@
     pack_w[...] = acc_w
     pack_e[...] = acc_e
 
-    pivot = fold_ref[0]
+    pivot = fold_buf[0]
     pivot_block, pivot_lane = lax.shift_right_logical(pivot, 7), pivot & (COLS - 1)
 
     @pl.when(top)
@@ -130,9 +131,20 @@
         choose = (source == ((pivot - target) & (COLS - 1))).astype(F32)
         turned = jnp.dot(fold_x[...], choose, precision=HIGHEST, preferred_element_type=F32)
         fold_src[...] = turned
-        fold_z[zi] = turned
+        fold_row[xi] = turned
+        fold_row[NX] = jnp.zeros_like(turned)
 
     pl.semaphore_wait(barrier, len(peers))
+
+    fold_x_copies = [
+        remote(fold_src, fold_row.at[xi], fx_send.at[d - 1], fx_recv.at[d - 1], lat, zi * NX + (xi + d) % NX)
+        for d in range(1, NX)
+    ]
+
+    @pl.when(top)
+    def _():
+        for d in far_first(NX):
+            fold_x_copies[d - 1].start()
 
     to_north = remote(raw_m.at[:, pl.ds(160, 16), :], raw_m.at[:, pl.ds(0, 16), :],
                       halo_send.at[0], halo_recv.at[0], north, lon)
@@ -145,18 +157,6 @@
     to_se = remote(pack_e.at[pl.ds(0, 16), :], corner.at[2], halo_send.at[6], halo_recv.at[6], south, east)
     to_sw = remote(pack_w.at[pl.ds(0, 16), :], corner.at[3], halo_send.at[7], halo_recv.at[7], south, west)
 
-    fold_z_copies = []
-    for d in range(1, NZ):
-        peer = (zi + d) % NZ
-        fold_z_copies.append(
-            remote(fold_src, fold_z.at[zi], fz_send.at[d - 1], fz_recv.at[d - 1], lat, peer * NX + xi)
-        )
-
-    @pl.when(top)
-    def _():
-        for d in far_first(NZ):
-            fold_z_copies[d - 1].start()
-
     @pl.when(jnp.logical_not(top))
     def _():
         to_ne.start()
@@ -171,52 +171,6 @@
 
     to_east.start()
     to_west.start()
-
-    def fold_want(xt):
-        want = (pivot_block - zi * NX - xt) & (LON - 1)
-        return want
-
-    @pl.when(top)
-    def _():
-        for d in range(1, NZ):
-            fold_z_copies[d - 1].wait_recv()
-        picks = []
-        for d in range(NX):
-            xt = (xi + d) % NX
-            ahead = fold_want(xt) + 1
-            block = ahead - ((ahead - xi) & (NX - 1))
-            picks.append(fold_z[lax.shift_right_logical(block & (LON - 1), 2)])
-        fold_got[xi] = picks[0]
-        copies = []
-        for d in range(1, NX):
-            fold_send[d] = picks[d]
-        for d in range(1, NX):
-            copy = remote(fold_send.at[d], fold_got.at[xi], fx_send.at[d - 1], fx_recv.at[d - 1],
-                          lat, zi * NX + (xi + d) % NX)
-            copy.start()
-            copies.append(copy)
-        for copy in copies:
-            copy.wait_recv()
-        want = fold_want(xi)
-        ahead2, here2, behind, behind2 = (
-            fold_got[(want + 1) & 3], fold_got[want & 3], fold_got[(want - 1) & 3], fold_got[(want - 2) & 3]
-        )
-        lane = lanes_of((32, COLS))
-        near = lane <= pivot_lane
-        ghost_m = jnp.where(near, here2, behind)
-        ghost_e = jnp.where(near, behind, behind2)
-        ghost_w = jnp.where(near, ahead2, here2)
-        ghost_h = jnp.where(lane < 9, ghost_e, jnp.where(lane >= 119, ghost_w, 0.0))
-        for ref, ghost in ((raw_m, ghost_m), (raw_h, ghost_h)):
-            for f in range(3):
-                ref[f, 176:192, :] = jnp.zeros((16, COLS), F32)
-            ref[0, 176:185, :] = ghost[0:9]
-            ref[1, 176:184, :] = ghost[9:17]
-            ref[2, 176:184, :] = ghost[17:25]
-        for copy in copies:
-            copy.wait_send()
-        for copy in fold_z_copies:
-            copy.wait_send()
 
     to_east.wait()
     to_west.wait()
@@ -230,6 +184,46 @@
             raw_h[f, 16 + 40 * g : 56 + 40 * g, :] = jnp.where(
                 lane40 < 9, near_e, jnp.where(lane40 >= 119, near_w, 0.0)
             )
+
+    for d in far_first(NZ):
+        pl.semaphore_signal(
+            plane_sem, inc=1, device_id={"lat": lat, "lon": ((zi + d) % NZ) * NX + xi},
+            device_id_type=pl.DeviceIdType.MESH,
+        )
+
+    fold_z_copies = [
+        remote(fold_send.at[d], fold_got.at[zi], fz_send.at[d - 1], fz_recv.at[d - 1],
+               lat, ((zi + d) % NZ) * NX + xi)
+        for d in range(1, NZ)
+    ]
+    lane32 = lanes_of((32, COLS))
+    near = lane32 <= pivot_lane
+
+    @pl.when(top)
+    def _():
+        for copy in fold_x_copies:
+            copy.wait_recv()
+        for d in far_first(NZ) + [0]:
+            want = pivot_block - ((zi + d) % NZ) * NX - xi
+
+            def block(b):
+                mine = (lax.shift_right_logical(b & (LON - 1), 2) == zi)
+                return fold_row[jnp.where(mine, b & (NX - 1), NX)]
+
+            ahead, here, behind, beyond = (block(want + o) for o in (1, 0, -1, -2))
+            window = jnp.where(near, here, behind)
+            edge = jnp.where(
+                lane32 < 9, jnp.where(near, behind, beyond),
+                jnp.where(lane32 >= 119, jnp.where(near, ahead, here), 0.0),
+            )
+            edges = sum(pltpu.roll(edge[8 * g : 8 * g + 8], 16 + 32 * g, 1) for g in range(4))
+            if d:
+                fold_send[d, 0:32, :] = window
+                fold_send[d, 32:40, :] = edges
+                fold_z_copies[d - 1].start()
+            else:
+                fold_got[zi, 0:32, :] = window
+                fold_got[zi, 32:40, :] = edges
 
     @pl.when(jnp.logical_not(bottom))
     def _():
@@ -251,77 +245,65 @@
             raw_m[f, 0:16, :] = jnp.zeros((16, COLS), F32)
             raw_h[f, 0:16, :] = jnp.zeros((16, COLS), F32)
 
-    @pl.when(jnp.logical_not(top))
-    def _():
-        to_ne.wait_send()
-        to_nw.wait_send()
-        to_north.wait_send()
-        to_se.wait_recv()
-        to_sw.wait_recv()
-        to_south.wait_recv()
-        for f in range(3):
-            at = 9 * f
-            near_e = pltpu.roll(corner[3], (COLS - at) % COLS, 1) if at else corner[3]
-            near_w = pltpu.roll(corner[2], (119 - at) % COLS, 1)
-            raw_h[f, 176:192, :] = jnp.where(lane16 < 9, near_e, jnp.where(lane16 >= 119, near_w, 0.0))
-
-    for r, n in chunks():
-        sums = []
-        for raw in (raw_m, raw_h):
-            up, mid, low = (raw[0, r + o : r + o + n, :] for o in (1, 0, -1))
-            both = up + low
-            wets = [(v > 0.0).astype(F32) for v in (up, mid, low)]
-            both_wet = wets[0] + wets[2]
-            sums.append((mid, both, mid + 0.5 * both, wets[1], both_wet, wets[1] + 0.5 * both_wet))
-        (dm, bm, cm, wm, bwm, cwm), (dh, bh, ch, wh, bwh, cwh) = sums
-        e_m, e_h = from_east(cm, ch)
-        w_m_, w_h_ = from_west(cm, ch)
-        ew_m, ew_h = from_east(cwm, cwh)
-        ww_m, ww_h = from_west(cwm, cwh)
-        rooted = []
-        for depth, wet, all_depth, all_wet in (
-            (dm, wm, bm + (e_m + w_m_), bwm + (ew_m + ww_m)),
-            (dh, wh, bh + (e_h + w_h_), bwh + (ew_h + ww_h)),
-        ):
-            links = 0.5 * (depth * all_wet + all_depth)
-            diagonal = wet * (depth * (1.0 / (REACH * REACH)) + links) + (1.0 - wet)
-            rooted.append(wet * lax.rsqrt(diagonal))
-        s_m[r : r + n, :], s_h[r : r + n, :] = rooted
-        se_m[r : r + n, :], se_h[r : r + n, :] = from_east(*rooted)
-        de_m[r : r + n, :], de_h[r : r + n, :] = from_east(dm, dh)
-        b_m[0, r : r + n, :] = wm * raw_m[2, r : r + n, :]
-        b_h[0, r : r + n, :] = wh * raw_h[2, r : r + n, :]
-        b_m[FIRST, r : r + n, :] = wm * raw_m[1, r : r + n, :]
-        b_h[FIRST, r : r + n, :] = wh * raw_h[1, r : r + n, :]
-
-    for r, n in chunks():
-        made = []
-        for raw, s, de, se, w in ((raw_m, s_m, de_m, se_m, w_m), (raw_h, s_h, de_h, se_h, w_h)):
-            d0, d1 = raw[0, r : r + n, :], raw[0, r + 1 : r + 1 + n, :]
-            s0, s1 = s[r : r + n, :], s[r + 1 : r + 1 + n, :]
-            de0, de1 = de[r : r + n, :], de[r + 1 : r + 1 + n, :]
-            se0, se1 = se[r : r + n, :], se[r + 1 : r + 1 + n, :]
-            east_w = -(d0 + de0) * (s0 * se0)
-            ne_w = -0.5 * (d0 + de1) * (s0 * se1)
-            nw_e = -0.5 * (de0 + d1) * (se0 * s1)
-            w[0, r : r + n, :] = -(d0 + d1) * (s0 * s1)
-            w[1, r : r + n, :] = east_w
-            w[3, r : r + n, :] = ne_w
-            w[6, r : r + n, :] = nw_e
-            made.append((east_w, ne_w, nw_e))
-        for slot, item in ((2, 0), (4, 1), (5, 2)):
-            w_m[slot, r : r + n, :], w_h[slot, r : r + n, :] = from_west(made[0][item], made[1][item])
+    def fields(spans):
+        for r, n in spans:
+            for raw, b in ((raw_m, b_m), (raw_h, b_h)):
+                wet = (raw[0, r : r + n, :] > 0.0).astype(F32)
+                b[0, r : r + n, :] = wet * raw[2, r : r + n, :]
+                b[FIRST, r : r + n, :] = wet * raw[1, r : r + n, :]
+
+    def roots(spans):
+        for r, n in spans:
+            sums = []
+            for raw in (raw_m, raw_h):
+                up, mid, low = (raw[0, r + o : r + o + n, :] for o in (1, 0, -1))
+                both = up + low
+                wets = [(v > 0.0).astype(F32) for v in (up, mid, low)]
+                both_wet = wets[0] + wets[2]
+                sums.append((mid, both, mid + 0.5 * both, wets[1], both_wet, wets[1] + 0.5 * both_wet))
+            (dm, bm, cm, wm, bwm, cwm), (dh, bh, ch, wh, bwh, cwh) = sums
+            e_m, e_h = from_east(cm, ch)
+            w_m_, w_h_ = from_west(cm, ch)
+            ew_m, ew_h = from_east(cwm, cwh)
+            ww_m, ww_h = from_west(cwm, cwh)
+            rooted = []
+            for depth, wet, all_depth, all_wet in (
+                (dm, wm, bm + (e_m + w_m_), bwm + (ew_m + ww_m)),
+                (dh, wh, bh + (e_h + w_h_), bwh + (ew_h + ww_h)),
+            ):
+                links = 0.5 * (depth * all_wet + all_depth)
+                diagonal = wet * (depth * (1.0 / (REACH * REACH)) + links) + (1.0 - wet)
+                rooted.append(wet * lax.rsqrt(diagonal))
+            s_m[r : r + n, :], s_h[r : r + n, :] = rooted
+            se_m[r : r + n, :], se_h[r : r + n, :] = from_east(*rooted)
+            de_m[r : r + n, :], de_h[r : r + n, :] = from_east(dm, dh)
+
+    def links(spans):
+        for r, n in spans:
+            made = []
+            for raw, s, de, se, w in ((raw_m, s_m, de_m, se_m, w_m), (raw_h, s_h, de_h, se_h, w_h)):
+                d0, d1 = raw[0, r : r + n, :], raw[0, r + 1 : r + 1 + n, :]
+                s0, s1 = s[r : r + n, :], s[r + 1 : r + 1 + n, :]
+                de0, de1 = de[r : r + n, :], de[r + 1 : r + 1 + n, :]
+                se0, se1 = se[r : r + n, :], se[r + 1 : r + 1 + n, :]
+                east_w = -(d0 + de0) * (s0 * se0)
+                ne_w = -0.5 * (d0 + de1) * (s0 * se1)
+                nw_e = -0.5 * (de0 + d1) * (se0 * s1)
+                w[0, r : r + n, :] = -(d0 + d1) * (s0 * s1)
+                w[1, r : r + n, :] = east_w
+                w[3, r : r + n, :] = ne_w
+                w[6, r : r + n, :] = nw_e
+                made.append((east_w, ne_w, nw_e))
+            for slot, item in ((2, 0), (4, 1), (5, 2)):
+                w_m[slot, r : r + n, :], w_h[slot, r : r + n, :] = from_west(made[0][item], made[1][item])
 
     def fold8(x):
         return sum(x[8 * k : 8 * k + 8] for k in range(x.shape[0] // 8))
 
-    def row_slices(r, n):
-        return max(r, 16) - r, min(r + n, 16 + ROWS) - r
-
-    def step(n, both, first):
+    def step(n, both, first, spans, gram_rows, add):
         bases = (0, FIRST) if both else (0,)
         total = [jnp.zeros((8, COLS), F32) for _ in range(6)]
-        for r, size in chunks():
+        for r, size in spans:
             weights = []
             for w in (w_m, w_h):
                 weights.append((
@@ -354,7 +336,7 @@
                 b_h[base + n, r : r + size, :] = out_h
                 news.append(out_m)
                 olds.append(mid_m)
-            lo, hi = row_slices(r, size)
+            lo, hi = max(r, gram_rows[0]) - r, min(r + size, gram_rows[1]) - r
             if hi > lo:
                 p1, p0 = news[0][lo:hi], olds[0][lo:hi]
                 total[0] = total[0] + fold8(p1 * p1)
@@ -368,8 +350,22 @@
                     r0 = b_m[FIRST + STEPS - 1, r + lo : r + hi, :]
                 total[5] = total[5] + fold8(p1 * r0)
         for c in range(6):
-            rows_acc[pl.ds(6 * n + c, 1), :] = jnp.sum(total[c], axis=0, keepdims=True)
-
+            row = jnp.sum(total[c], axis=0, keepdims=True)
+            at = pl.ds(6 * n + c, 1)
+            rows_acc[at, :] = rows_acc[at, :] + row if add else row
+
+    def steps(spans, gram_rows, add):
+        step(1, True, True, spans, gram_rows, add)
+
+        @pl.loop(2, STEPS)
+        def _(n):
+            step(n, True, False, spans, gram_rows, add)
+
+        step(STEPS, False, False, spans, gram_rows, add)
+
+    fields(chunks(LO, 176))
+    roots(chunks(LO, 168) + [(168, 7)])
+    links(chunks(LO, 168))
     start = [jnp.zeros((8, COLS), F32) for _ in range(3)]
     for r in range(16, 16 + ROWS, CHUNK):
         p0, r0 = b_m[0, r : r + CHUNK, :], b_m[FIRST, r : r + CHUNK, :]
@@ -377,20 +373,49 @@
     for c in range(3):
         rows_acc[2 * c : 2 * c + 1, :] = jnp.sum(start[c], axis=0, keepdims=True)
 
-    step(1, True, True)
-
-    @pl.loop(2, STEPS)
-    def _(n):
-        step(n, True, False)
-
-    step(STEPS, False, False)
-
-    outs = [
-        pltpu.make_async_copy(b_m.at[k, pl.ds(16, ROWS), :], basis_out.at[k], out_sem.at[k])
-        for k in range(FIELDS)
-    ]
-    for copy in outs:
-        copy.start()
+    steps(chunks(LO, 168), (16, 160), False)
+
+    @pl.when(jnp.logical_not(top))
+    def _():
+        to_ne.wait_send()
+        to_nw.wait_send()
+        to_north.wait_send()
+        to_se.wait_recv()
+        to_sw.wait_recv()
+        to_south.wait_recv()
+        for f in range(3):
+            at = 9 * f
+            near_e = pltpu.roll(corner[3], (COLS - at) % COLS, 1) if at else corner[3]
+            near_w = pltpu.roll(corner[2], (119 - at) % COLS, 1)
+            raw_h[f, 176:192, :] = jnp.where(lane16 < 9, near_e, jnp.where(lane16 >= 119, near_w, 0.0))
+
+    @pl.when(top)
+    def _():
+        for copy in fold_z_copies:
+            copy.wait_recv()
+        ghost = fold_got[0]
+        for k in range(1, NZ):
+            ghost = ghost + fold_got[k]
+        edges = ghost[32:40]
+        lane8 = lanes_of((8, COLS))
+        side = []
+        for g in range(4):
+            edge = pltpu.roll(edges, (COLS - 16 - 32 * g) % COLS, 1)
+            side.append(jnp.where((lane8 < 9) | (lane8 >= 119), edge, 0.0))
+        side = jnp.concatenate(side, axis=0)
+        for ref, got in ((raw_m, ghost), (raw_h, side)):
+            for f in range(3):
+                ref[f, 176:192, :] = jnp.zeros((16, COLS), F32)
+            ref[0, 176:185, :] = got[0:9]
+            ref[1, 176:184, :] = got[9:17]
+            ref[2, 176:184, :] = got[17:25]
+        for copy in fold_x_copies + fold_z_copies:
+            copy.wait_send()
+
+    fields([(176, 8)])
+    roots([(168, 16)])
+    links([(168, 16)])
+    steps([(160, 24)], (160, 176), True)
 
     ones = jnp.ones((8, COLS), F32)
     sums = lax.dot_general(
@@ -408,25 +433,25 @@
             copies[d - 1].start()
         for copy in copies:
             copy.wait_recv()
-        total = slots[0]
-        for k in range(1, count):
-            total = total + slots[k]
-        return total, copies
-
+        terms = [slots[k] for k in range(count)]
+        while len(terms) > 1:
+            terms = [a + b for a, b in zip(terms[::2], terms[1::2])]
+        return terms[0], copies
+
+    pl.semaphore_wait(plane_sem, NZ - 1)
     sums, first_copies = reduce(
-        0, sums, red_x, rx_send, rx_recv, NX, xi,
-        lambda d: (lat, zi * NX + (xi + d) % NX), far_first(NX))
+        0, sums, red_p, rp_send, rp_recv, LON, lon,
+        lambda d: (lat, (lon + d) % LON), far_first(LON))
     sums, second_copies = reduce(
-        1, sums, red_z, rz_send, rz_recv, NZ, zi,
-        lambda d: (lat, ((zi + d) % NZ) * NX + xi), far_first(NZ))
-    sums, third_copies = reduce(
-        2, sums, red_y, ry_send, ry_recv, LAT, lat,
+        1, sums, red_y, ry_send, ry_recv, LAT, lat,
         lambda d: ((lat + d) % LAT, lon), far_first(LAT))
     moments_out[...] = sums
-    for copy in first_copies + second_copies + third_copies:
+    for copy in first_copies + second_copies:
         copy.wait_send()
-    for copy in outs:
-        copy.wait()
+
+
+def held(shape):
+    return pltpu.VMEM(shape, F32)
 
 
 def basis_and_moments(forcing, search, depth, mask, fold_map):
@@ -435,35 +460,27 @@
     ext = (EXT, COLS)
     return pl.pallas_call(
         basis_kernel,
-        grid=(1,),
-        out_shape=(
-            jax.ShapeDtypeStruct((FIELDS, ROWS, COLS), F32),
-            jax.ShapeDtypeStruct((1, COLS), F32),
-        ),
-        in_specs=[pl.BlockSpec((1024,), lambda i: (0,), memory_space=pltpu.SMEM)]
-        + [pl.BlockSpec(memory_space=pl.ANY)] * 4,
-        out_specs=(
-            pl.BlockSpec(memory_space=pl.ANY),
-            pl.BlockSpec((1, COLS), lambda i: (0, 0)),
-        ),
+        out_shape=(held((FIELDS,) + ext), held((1, COLS))),
+        in_specs=[pl.BlockSpec(memory_space=pl.ANY)] * 5,
+        out_specs=(pl.BlockSpec(memory_space=vm), pl.BlockSpec(memory_space=vm)),
         scratch_shapes=[
+            pltpu.SMEM((1024,), jnp.int32),
             vm((3,) + ext, F32), vm((3,) + ext, F32),
             vm((ROWS, COLS), F32), vm((ROWS, COLS), jnp.int32),
             vm((40, COLS), F32), vm((40, COLS), F32), vm((40, COLS), F32), vm((40, COLS), F32),
             vm((4, 16, COLS), F32),
-            vm((32, COLS), F32), vm((32, COLS), F32), vm((NZ, 32, COLS), F32),
-            vm((NX, 32, COLS), F32), vm((NX, 32, COLS), F32),
+            vm((32, COLS), F32), vm((32, COLS), F32), vm((NX + 1, 32, COLS), F32),
+            vm((NZ, 40, COLS), F32), vm((NZ, 40, COLS), F32),
         ]
         + [vm(ext, F32)] * 8
         + [vm((7,) + ext, F32)] * 2
-        + [vm((FIELDS,) + ext, F32)] * 2
+        + [vm((FIELDS,) + ext, F32)]
         + [
-            vm((COLS, COLS), F32), vm((3, 1, COLS), F32),
-            vm((NX, 1, COLS), F32), vm((NZ, 1, COLS), F32), vm((LAT, 1, COLS), F32),
-            dma((4,)), dma((FIELDS,)), dma((8,)), dma((8,)),
+            vm((COLS, COLS), F32), vm((2, 1, COLS), F32),
+            vm((LON, 1, COLS), F32), vm((LAT, 1, COLS), F32),
+            pltpu.SemaphoreType.REGULAR, dma((5,)), dma((8,)), dma((8,)),
             dma((NZ - 1,)), dma((NZ - 1,)), dma((NX - 1,)), dma((NX - 1,)),
-            dma((NX - 1,)), dma((NX - 1,)), dma((NZ - 1,)), dma((NZ - 1,)),
-            dma((LAT - 1,)), dma((LAT - 1,)),
+            dma((LON - 1,)), dma((LON - 1,)), dma((LAT - 1,)), dma((LAT - 1,)),
         ],
         compiler_params=pltpu.CompilerParams(collective_id=0, has_side_effects=True),
         name="basis",
@@ -549,7 +566,7 @@
         height = jnp.zeros((size, COLS), F32)
         residual = jnp.zeros((size, COLS), F32)
         for k in range(FIELDS):
-            field = basis_ref[k, at : at + size, :]
+            field = basis_ref[k, 16 + at : 16 + at + size, :]
             height = height + x_s[k : k + 1, :] * field
             residual = residual + r_s[k : k + 1, :] * field
         height_ref[at : at + size, :] = height
@@ -558,10 +575,12 @@
 
 def per_device(forcing, search, depth, mask, fold_map):
     basis, moments = basis_and_moments(forcing, search, depth, mask, fold_map)
+    basis, moments = (pltpu.with_memory_space_constraint(v, pltpu.VMEM) for v in (basis, moments))
     block = jax.ShapeDtypeStruct((ROWS, COLS), F32)
     return pl.pallas_call(
         combine_kernel,
         out_shape=(block, block),
+        in_specs=[pl.BlockSpec(memory_space=pltpu.VMEM)] * 2,
         name="combine",
     )(moments, basis)
 

time: 43.4 us -> 39.9 us (0.919)
  Pallas kernels: 42.5 us -> 39.1 us
    pallas_call x2, Pallas kernels: 42.5 us -> 39.1 us  [the longest x1 37 us: basis_and_moments(): pl.pallas_call(basis_kernel, out_shape=(held((FIELDS,) + ext), held((1, C...]
where the time goes in v1:
time: 39.9 us; the launch traced here: 39.7 us
  Pallas kernels  39.1 us (98%)
  between operations  0.64 us (2%)
    pallas_call x1, Pallas kernels, basis_and_moments(): pl.pallas_call(basis_kernel, out_shape=(held((FIELDS,) + ext), held((1, C...  37 us
    pallas_call x1, Pallas kernels, per_device(): pl.pallas_call(combine_kernel, out_shape=(block, block), in_specs=[pl.Blo...  2.08 us

profile of v1, /device:TPU:1, one launch (start us, length us, event | category | flops | bytes accessed | tf_op | source)
XLA Modules:
  0.0 39.7 jit_solution(18312132748732285352)
XLA Ops:
  0.6 37.0 %basis.1 = (f32[17,192,128]{2,1,0:T(8,128)S(1)}, f32[1,128]{1,0:T(1,128)S(1)}) custom-call(s32[4096]{0:T(1024)} %fold_ref.1, f32[160,128]{1,0:T(8,128)} %forcing_ref.1, f32[160,128]{1,0:T(8,128)} %search_ref.1, f32[160,128]{1,0:T(8,128)} %depth_ref.1, s32[160,128]{1,0:T(8,128)} %mask_ref.1), custom_call_target="tpu_custom_call" | custom-call | tf_op jit(solution)/shard_map/basis/pallas_call | solution.py:461
  37.6 2.1 %combine.1 = (f32[160,128]{1,0:T(8,128)}, f32[160,128]{1,0:T(8,128)}) custom-call(f32[1,128]{1,0:T(1,128)S(1)} %get-tuple-element.4.moments_ref, f32[17,192,128]{2,1,0:T(8,128)S(1)} %get-tuple-element.5.basis_ref), custom_call_target="tpu_custom_call" | custom-call | tf_op jit(solution)/shard_map/combine/pallas_call | solution.py:580

commit v2 on v1

--- a/solution.py
+++ b/solution.py
@@ -87,15 +87,44 @@
     ]
     for copy in loads:
         copy.start()
-    peers = [(lat, ((zi + d) % NZ) * NX + xi) for d in far_first(NZ)]
-    peers += [((lat + d) % LAT, lon) for d in far_first(LAT)]
-    peers += [(north, east), (north, west), (south, east), (south, west)]
-    peers += [(lat, zi * NX + (xi + d) % NX) for d in far_first(NX)]
-    peers += [(lat, east), (lat, west)]
-    for a, b in peers:
-        pl.semaphore_signal(
-            barrier, inc=1, device_id={"lat": a, "lon": b}, device_id_type=pl.DeviceIdType.MESH
-        )
+    def greet(semaphore, to):
+        for a, b in to:
+            pl.semaphore_signal(
+                semaphore, inc=1, device_id={"lat": a, "lon": b}, device_id_type=pl.DeviceIdType.MESH
+            )
+
+    fold_peers = [(lat, ((zi + d) % NZ) * NX + xi) for d in far_first(NZ)]
+    fold_peers += [(lat, zi * NX + (xi + d) % NX) for d in far_first(NX)]
+    beside = [(lat, east), (lat, west), (north, east), (north, west), (south, east), (south, west),
+              (north, lon), (south, lon)]
+
+    @pl.when(top)
+    def _():
+        greet(barrier, fold_peers)
+
+    greet(barrier, beside)
+
+    def distant(level):
+        far = 1 << level
+        to = [(lat, (lon + far) % LON), (lat, (lon + LON - far) % LON)]
+        if 2 * far <= LAT // 2:
+            to += [((lat + far) % LAT, lon), ((lat + LAT - far) % LAT, lon)]
+        return to
+
+    levels = 1
+    while (2 << (levels - 1)) < LON // 2:
+        levels += 1
+
+    passed = set()
+
+    def next_level(level):
+        if level > levels or level in passed:
+            return
+        passed.add(level)
+        if level > 0:
+            pl.semaphore_wait(plane_sem.at[level - 1], len(distant(level - 1)))
+        if level < levels:
+            greet(plane_sem.at[level], distant(level))
 
     rows_acc[...] = jnp.zeros_like(rows_acc)
     for copy in loads:
@@ -134,7 +163,7 @@
         fold_row[xi] = turned
         fold_row[NX] = jnp.zeros_like(turned)
 
-    pl.semaphore_wait(barrier, len(peers))
+    pl.semaphore_wait(barrier, len(beside) + jnp.where(top, len(fold_peers), 0))
 
     fold_x_copies = [
         remote(fold_src, fold_row.at[xi], fx_send.at[d - 1], fx_recv.at[d - 1], lat, zi * NX + (xi + d) % NX)
@@ -157,6 +186,10 @@
     to_se = remote(pack_e.at[pl.ds(0, 16), :], corner.at[2], halo_send.at[6], halo_recv.at[6], south, east)
     to_sw = remote(pack_w.at[pl.ds(0, 16), :], corner.at[3], halo_send.at[7], halo_recv.at[7], south, west)
 
+    to_east.start()
+    to_west.start()
+    next_level(0)
+
     @pl.when(jnp.logical_not(top))
     def _():
         to_ne.start()
@@ -168,9 +201,6 @@
         to_se.start()
         to_sw.start()
         to_south.start()
-
-    to_east.start()
-    to_west.start()
 
     to_east.wait()
     to_west.wait()
@@ -184,12 +214,6 @@
             raw_h[f, 16 + 40 * g : 56 + 40 * g, :] = jnp.where(
                 lane40 < 9, near_e, jnp.where(lane40 >= 119, near_w, 0.0)
             )
-
-    for d in far_first(NZ):
-        pl.semaphore_signal(
-            plane_sem, inc=1, device_id={"lat": lat, "lon": ((zi + d) % NZ) * NX + xi},
-            device_id_type=pl.DeviceIdType.MESH,
-        )
 
     fold_z_copies = [
         remote(fold_send.at[d], fold_got.at[zi], fz_send.at[d - 1], fz_recv.at[d - 1],
@@ -225,25 +249,7 @@
                 fold_got[zi, 0:32, :] = window
                 fold_got[zi, 32:40, :] = edges
 
-    @pl.when(jnp.logical_not(bottom))
-    def _():
-        to_se.wait_send()
-        to_sw.wait_send()
-        to_south.wait_send()
-        to_ne.wait_recv()
-        to_nw.wait_recv()
-        to_north.wait_recv()
-        for f in range(3):
-            at = 96 + 9 * f
-            near_e = pltpu.roll(corner[1], (COLS - at) % COLS, 1)
-            near_w = pltpu.roll(corner[0], (119 - at) % COLS, 1)
-            raw_h[f, 0:16, :] = jnp.where(lane16 < 9, near_e, jnp.where(lane16 >= 119, near_w, 0.0))
-
-    @pl.when(bottom)
-    def _():
-        for f in range(3):
-            raw_m[f, 0:16, :] = jnp.zeros((16, COLS), F32)
-            raw_h[f, 0:16, :] = jnp.zeros((16, COLS), F32)
+    next_level(1)
 
     def fields(spans):
         for r, n in spans:
@@ -300,10 +306,10 @@
     def fold8(x):
         return sum(x[8 * k : 8 * k + 8] for k in range(x.shape[0] // 8))
 
-    def step(n, both, first, spans, gram_rows, add):
+    def step(n, both, first, spans, add):
         bases = (0, FIRST) if both else (0,)
         total = [jnp.zeros((8, COLS), F32) for _ in range(6)]
-        for r, size in spans:
+        for r, size, gram_rows in spans:
             weights = []
             for w in (w_m, w_h):
                 weights.append((
@@ -354,18 +360,19 @@
             at = pl.ds(6 * n + c, 1)
             rows_acc[at, :] = rows_acc[at, :] + row if add else row
 
-    def steps(spans, gram_rows, add):
-        step(1, True, True, spans, gram_rows, add)
+    def steps(spans, add):
+        step(1, True, True, spans, add)
 
         @pl.loop(2, STEPS)
         def _(n):
-            step(n, True, False, spans, gram_rows, add)
-
-        step(STEPS, False, False, spans, gram_rows, add)
-
-    fields(chunks(LO, 176))
-    roots(chunks(LO, 168) + [(168, 7)])
-    links(chunks(LO, 168))
+            step(n, True, False, spans, add)
+
+        step(STEPS, False, False, spans, add)
+
+    fields(chunks(16, 176))
+    roots([(17, 7)] + chunks(24, 168) + [(168, 7)])
+    links(chunks(16, 168))
+    next_level(2)
     start = [jnp.zeros((8, COLS), F32) for _ in range(3)]
     for r in range(16, 16 + ROWS, CHUNK):
         p0, r0 = b_m[0, r : r + CHUNK, :], b_m[FIRST, r : r + CHUNK, :]
@@ -373,7 +380,28 @@
     for c in range(3):
         rows_acc[2 * c : 2 * c + 1, :] = jnp.sum(start[c], axis=0, keepdims=True)
 
-    steps(chunks(LO, 168), (16, 160), False)
+    steps([(r, n, (32, 160)) for r, n in chunks(16, 168)], False)
+    next_level(3)
+
+    @pl.when(jnp.logical_not(bottom))
+    def _():
+        to_se.wait_send()
+        to_sw.wait_send()
+        to_south.wait_send()
+        to_ne.wait_recv()
+        to_nw.wait_recv()
+        to_north.wait_recv()
+        for f in range(3):
+            at = 96 + 9 * f
+            near_e = pltpu.roll(corner[1], (COLS - at) % COLS, 1)
+            near_w = pltpu.roll(corner[0], (119 - at) % COLS, 1)
+            raw_h[f, 0:16, :] = jnp.where(lane16 < 9, near_e, jnp.where(lane16 >= 119, near_w, 0.0))
+
+    @pl.when(bottom)
+    def _():
+        for f in range(3):
+            raw_m[f, 0:16, :] = jnp.zeros((16, COLS), F32)
+            raw_h[f, 0:16, :] = jnp.zeros((16, COLS), F32)
 
     @pl.when(jnp.logical_not(top))
     def _():
@@ -412,11 +440,10 @@
         for copy in fold_x_copies + fold_z_copies:
             copy.wait_send()
 
-    fields([(176, 8)])
-    roots([(168, 16)])
-    links([(168, 16)])
-    steps([(160, 24)], (160, 176), True)
-
+    fields([(LO, 8), (176, 8)])
+    roots([(LO, 16), (168, 16)])
+    links([(LO, 16), (168, 16)])
+    steps([(LO, 24, (16, 32)), (160, 24, (160, 176))], True)
     ones = jnp.ones((8, COLS), F32)
     sums = lax.dot_general(
         ones, rows_acc[...], (((1,), (1,)), ((), ())), precision=HIGHEST, preferred_element_type=F32
@@ -438,13 +465,13 @@
             terms = [a + b for a, b in zip(terms[::2], terms[1::2])]
         return terms[0], copies
 
-    pl.semaphore_wait(plane_sem, NZ - 1)
     sums, first_copies = reduce(
-        0, sums, red_p, rp_send, rp_recv, LON, lon,
+        0, sums, red_y, ry_send, ry_recv, LAT, lat,
+        lambda d: ((lat + d) % LAT, lon), far_first(LAT))
+    next_level(levels)
+    sums, second_copies = reduce(
+        1, sums, red_p, rp_send, rp_recv, LON, lon,
         lambda d: (lat, (lon + d) % LON), far_first(LON))
-    sums, second_copies = reduce(
-        1, sums, red_y, ry_send, ry_recv, LAT, lat,
-        lambda d: ((lat + d) % LAT, lon), far_first(LAT))
     moments_out[...] = sums
     for copy in first_copies + second_copies:
         copy.wait_send()
@@ -478,7 +505,7 @@
         + [
             vm((COLS, COLS), F32), vm((2, 1, COLS), F32),
             vm((LON, 1, COLS), F32), vm((LAT, 1, COLS), F32),
-            pltpu.SemaphoreType.REGULAR, dma((5,)), dma((8,)), dma((8,)),
+            pltpu.SemaphoreType.REGULAR((4,)), dma((5,)), dma((8,)), dma((8,)),
             dma((NZ - 1,)), dma((NZ - 1,)), dma((NX - 1,)), dma((NX - 1,)),
             dma((LON - 1,)), dma((LON - 1,)), dma((LAT - 1,)), dma((LAT - 1,)),
         ],

time: 39.9 us -> 38 us (0.952)
  Pallas kernels: 39.1 us -> 37.2 us
    pallas_call x1, Pallas kernels: 37 us -> 35.2 us  [basis_and_moments(): pl.pallas_call(basis_kernel, out_shape=(held((FIELDS,) + ext), held((1, C...]
where the time goes in v2:
time: 38 us; the launch traced here: 37.9 us
  Pallas kernels  37.2 us (98%)
  between operations  0.64 us (2%)
    pallas_call x1, Pallas kernels, basis_and_moments(): pl.pallas_call(basis_kernel, out_shape=(held((FIELDS,) + ext), held((1, C...  35.2 us
    pallas_call x1, Pallas kernels, per_device(): pl.pallas_call(combine_kernel, out_shape=(block, block), in_specs=[pl.Blo...  2.08 us

profile of v2, /device:TPU:1, one launch (start us, length us, event | category | flops | bytes accessed | tf_op | source)
XLA Modules:
  0.0 37.9 jit_solution(999267273307314751)
XLA Ops:
  0.6 35.2 %basis.1 = (f32[17,192,128]{2,1,0:T(8,128)S(1)}, f32[1,128]{1,0:T(1,128)S(1)}) custom-call(s32[4096]{0:T(1024)} %fold_ref.1, f32[160,128]{1,0:T(8,128)} %forcing_ref.1, f32[160,128]{1,0:T(8,128)} %search_ref.1, f32[160,128]{1,0:T(8,128)} %depth_ref.1, s32[160,128]{1,0:T(8,128)} %mask_ref.1), custom_call_target="tpu_custom_call" | custom-call | tf_op jit(solution)/shard_map/basis/pallas_call | solution.py:488
  35.8 2.1 %combine.1 = (f32[160,128]{1,0:T(8,128)}, f32[160,128]{1,0:T(8,128)}) custom-call(f32[1,128]{1,0:T(1,128)S(1)} %get-tuple-element.4.moments_ref, f32[17,192,128]{2,1,0:T(8,128)S(1)} %get-tuple-element.5.basis_ref), custom_call_target="tpu_custom_call" | custom-call | tf_op jit(solution)/shard_map/combine/pallas_call | solution.py:607

commit v3 on v2

--- a/solution.py
+++ b/solution.py
@@ -94,9 +94,18 @@
             )
 
     fold_peers = [(lat, ((zi + d) % NZ) * NX + xi) for d in far_first(NZ)]
-    fold_peers += [(lat, zi * NX + (xi + d) % NX) for d in far_first(NX)]
-    beside = [(lat, east), (lat, west), (north, east), (north, west), (south, east), (south, west),
-              (north, lon), (south, lon)]
+
+    def around(far):
+        if 2 * far == NZ:
+            return [(lat, (lon + NX * far) % LON)]
+        to = [(lat, (lon + NX * far) % LON), (lat, (lon + LON - NX * far) % LON)]
+        if 2 * far < LAT:
+            to += [((lat + 2 * far) % LAT, lon), ((lat + LAT - 2 * far) % LAT, lon)]
+        return to
+
+    beside = [(lat, zi * NX + (xi + d) % NX) for d in far_first(NX)]
+    beside += [(north, east), (north, west), (south, east), (south, west)]
+    beside += [(lat, east), (lat, west), (north, lon), (south, lon)] + around(1)
 
     @pl.when(top)
     def _():
@@ -104,27 +113,13 @@
 
     greet(barrier, beside)
 
-    def distant(level):
-        far = 1 << level
-        to = [(lat, (lon + far) % LON), (lat, (lon + LON - far) % LON)]
-        if 2 * far <= LAT // 2:
-            to += [((lat + far) % LAT, lon), ((lat + LAT - far) % LAT, lon)]
-        return to
-
-    levels = 1
-    while (2 << (levels - 1)) < LON // 2:
-        levels += 1
-
-    passed = set()
+    levels = 3
 
     def next_level(level):
-        if level > levels or level in passed:
-            return
-        passed.add(level)
         if level > 0:
-            pl.semaphore_wait(plane_sem.at[level - 1], len(distant(level - 1)))
+            pl.semaphore_wait(plane_sem.at[level - 1], len(around(1 << (level - 1))))
         if level < levels:
-            greet(plane_sem.at[level], distant(level))
+            greet(plane_sem.at[level], around(1 << level))
 
     rows_acc[...] = jnp.zeros_like(rows_acc)
     for copy in loads:
@@ -372,7 +367,6 @@
     fields(chunks(16, 176))
     roots([(17, 7)] + chunks(24, 168) + [(168, 7)])
     links(chunks(16, 168))
-    next_level(2)
     start = [jnp.zeros((8, COLS), F32) for _ in range(3)]
     for r in range(16, 16 + ROWS, CHUNK):
         p0, r0 = b_m[0, r : r + CHUNK, :], b_m[FIRST, r : r + CHUNK, :]
@@ -381,7 +375,7 @@
         rows_acc[2 * c : 2 * c + 1, :] = jnp.sum(start[c], axis=0, keepdims=True)
 
     steps([(r, n, (32, 160)) for r, n in chunks(16, 168)], False)
-    next_level(3)
+    next_level(2)
 
     @pl.when(jnp.logical_not(bottom))
     def _():

time: 38 us -> 37.6 us (0.989)
  Pallas kernels: 37.2 us -> 36.8 us
    pallas_call x1, Pallas kernels: 35.2 us -> 34.7 us  [basis_and_moments(): pl.pallas_call(basis_kernel, out_shape=(held((FIELDS,) + ext), held((1, C...]
where the time goes in v3:
time: 37.6 us; the launch traced here: 37.5 us
  Pallas kernels  36.8 us (98%)
  between operations  0.64 us (2%)
    pallas_call x1, Pallas kernels, basis_and_moments(): pl.pallas_call(basis_kernel, out_shape=(held((FIELDS,) + ext), held((1, C...  34.7 us
    pallas_call x1, Pallas kernels, per_device(): pl.pallas_call(combine_kernel, out_shape=(block, block), in_specs=[pl.Blo...  2.08 us

profile of v3, /device:TPU:1, one launch (start us, length us, event | category | flops | bytes accessed | tf_op | source)
XLA Modules:
  0.0 37.5 jit_solution(10028660534074813801)
XLA Ops:
  0.6 34.7 %basis.1 = (f32[17,192,128]{2,1,0:T(8,128)S(1)}, f32[1,128]{1,0:T(1,128)S(1)}) custom-call(s32[4096]{0:T(1024)} %fold_ref.1, f32[160,128]{1,0:T(8,128)} %forcing_ref.1, f32[160,128]{1,0:T(8,128)} %search_ref.1, f32[160,128]{1,0:T(8,128)} %depth_ref.1, s32[160,128]{1,0:T(8,128)} %mask_ref.1), custom_call_target="tpu_custom_call" | custom-call | tf_op jit(solution)/shard_map/basis/pallas_call | solution.py:482
  35.4 2.1 %combine.1 = (f32[160,128]{1,0:T(8,128)}, f32[160,128]{1,0:T(8,128)}) custom-call(f32[1,128]{1,0:T(1,128)S(1)} %get-tuple-element.4.moments_ref, f32[17,192,128]{2,1,0:T(8,128)S(1)} %get-tuple-element.5.basis_ref), custom_call_target="tpu_custom_call" | custom-call | tf_op jit(solution)/shard_map/combine/pallas_call | solution.py:601

commit v4 on v3

v4 whole, which is shorter than its diff:
```python
import functools

import jax
import jax.numpy as jnp
from jax import lax
from jax.experimental import pallas as pl
from jax.experimental.pallas import tpu as pltpu
from jax.sharding import PartitionSpec as P

STEPS = 8
REACH = 256
LAT, LON, NX, NZ = 16, 32, 4, 8
ROWS, COLS = 160, 128
EXT = ROWS + 32
LO = 8
FIELDS = 2 * STEPS + 1
FIRST = STEPS + 1
HIGHEST = lax.Precision.HIGHEST
F32 = jnp.float32


def lanes_of(shape):
    return lax.broadcasted_iota(jnp.int32, shape, len(shape) - 1)


def from_east(x):
    return pltpu.roll(x, COLS - 1, 1)


def from_west(x):
    return pltpu.roll(x, 1, 1)


def shift(x, by):
    by %= COLS
    return pltpu.roll(x, by, 1) if by else x


WEST = 28


def strip_lanes(lane, half):
    lane = (lane - half) & (COLS - 1)
    return (lane >= 119) | ((lane >= WEST) & (lane < WEST + 9))


def within(lane, start, stop):
    return (lane >= start) & (lane < stop)


def remote(src, dst, send, recv, lat, lon):
    return pltpu.make_async_remote_copy(
        src_ref=src,
        dst_ref=dst,
        send_sem=send,
        recv_sem=recv,
        device_id={"lat": lat, "lon": lon},
        device_id_type=pl.DeviceIdType.MESH,
    )


CHUNK = 16


def far_first(count):
    return sorted(range(1, count), key=lambda d: (-min(d, count - d), d))


def chunks(start, stop):
    return [(r, min(CHUNK, stop - r)) for r in range(start, stop, CHUNK)]


def basis_kernel(
    fold_ref, forcing_ref, search_ref, depth_ref, mask_ref,
    b_m, b_s, moments_out,
    fold_buf, raw_m, side_depth, side_state, depth_buf, mask_buf, pack_w, pack_e, got_w, got_e, corner,
    fold_x, fold_src, fold_row, fold_send, fold_got,
    s_m, s_s, de_m, de_s, se_m, se_s,
    w_m, w_s, rows_acc, part, red_p, red_y,
    plane_sem, local_sem, halo_send, halo_recv, fz_send, fz_recv, fx_send, fx_recv,
    rp_send, rp_recv, ry_send, ry_recv,
):
    lat = lax.axis_index("lat")
    lon = lax.axis_index("lon")
    zi, xi = lon // NX, lon % NX
    top = lat == LAT - 1
    bottom = lat == 0
    north, south = (lat + 1) % LAT, (lat + LAT - 1) % LAT
    east, west = (lon + 1) % LON, (lon + LON - 1) % LON
    barrier = pltpu.get_barrier_semaphore()

    loads = [
        pltpu.make_async_copy(depth_ref, depth_buf, local_sem.at[0]),
        pltpu.make_async_copy(mask_ref, mask_buf, local_sem.at[1]),
        pltpu.make_async_copy(forcing_ref, raw_m.at[1, pl.ds(16, ROWS), :], local_sem.at[2]),
        pltpu.make_async_copy(search_ref, raw_m.at[2, pl.ds(16, ROWS), :], local_sem.at[3]),
        pltpu.make_async_copy(fold_ref.at[pl.ds(0, 1024)], fold_buf, local_sem.at[4]),
    ]
    for copy in loads:
        copy.start()

    def greet(semaphore, to):
        for a, b in to:
            pl.semaphore_signal(
                semaphore, inc=1, device_id={"lat": a, "lon": b}, device_id_type=pl.DeviceIdType.MESH
            )

    def around(far):
        if 2 * far == NZ:
            return [(lat, (lon + NX * far) % LON)]
        to = [(lat, (lon + NX * far) % LON), (lat, (lon + LON - NX * far) % LON)]
        if 2 * far < LAT:
            to += [((lat + 2 * far) % LAT, lon), ((lat + LAT - 2 * far) % LAT, lon)]
        return to

    beside = [(lat, zi * NX + (xi + d) % NX) for d in far_first(NX)]
    beside += [(north, east), (north, west), (south, east), (south, west)]
    beside += [(lat, east), (lat, west), (north, lon), (south, lon)] + around(1)

    greet(barrier, beside)

    levels = 3

    def next_level(level):
        if level > 0:
            pl.semaphore_wait(plane_sem.at[level - 1], len(around(1 << (level - 1))))
        if level < levels:
            greet(plane_sem.at[level], around(1 << level))

    rows_acc[...] = jnp.zeros_like(rows_acc)
    for copy in loads:
        copy.wait()
    raw_m[0, 16 : 16 + ROWS, :] = depth_buf[...] * mask_buf[...].astype(F32)

    lane40 = lanes_of((40, COLS))
    acc_w = jnp.zeros((40, COLS), F32)
    acc_e = jnp.zeros((40, COLS), F32)
    for g in range(4):
        for f in range(3):
            at = 32 * g + 9 * f
            block = raw_m[f, 16 + 40 * g : 56 + 40 * g, :]
            here = (lane40 >= at) & (lane40 < at + 9)
            acc_w = jnp.where(here, pltpu.roll(block, at, 1) if at else block, acc_w)
            acc_e = jnp.where(here, pltpu.roll(block, (at - 119) % COLS, 1), acc_e)
    pack_w[...] = acc_w
    pack_e[...] = acc_e

    pivot = fold_buf[0]
    pivot_block, pivot_lane = lax.shift_right_logical(pivot, 7), pivot & (COLS - 1)

    @pl.when(top)
    def _():
        fold_x[...] = jnp.zeros_like(fold_x)
        for m in range(9):
            fold_x[m : m + 1, :] = raw_m[0, 175 - m : 176 - m, :]
        for m in range(8):
            fold_x[9 + m : 10 + m, :] = raw_m[1, 175 - m : 176 - m, :]
            fold_x[17 + m : 18 + m, :] = raw_m[2, 175 - m : 176 - m, :]
        source = lax.broadcasted_iota(jnp.int32, (COLS, COLS), 0)
        target = lax.broadcasted_iota(jnp.int32, (COLS, COLS), 1)
        choose = (source == ((pivot - target) & (COLS - 1))).astype(F32)
        turned = jnp.dot(fold_x[...], choose, precision=HIGHEST, preferred_element_type=F32)
        fold_src[...] = turned
        fold_row[xi] = turned
        fold_row[NX] = jnp.zeros_like(turned)

    pl.semaphore_wait(barrier, len(beside))

    fold_x_copies = [
        remote(fold_src, fold_row.at[xi], fx_send.at[d - 1], fx_recv.at[d - 1], lat, zi * NX + (xi + d) % NX)
        for d in range(1, NX)
    ]

    @pl.when(top)
    def _():
        for d in far_first(NX):
            fold_x_copies[d - 1].start()

    to_north = remote(raw_m.at[:, pl.ds(160, 16), :], raw_m.at[:, pl.ds(0, 16), :],
                      halo_send.at[0], halo_recv.at[0], north, lon)
    to_south = remote(raw_m.at[:, pl.ds(16, 16), :], raw_m.at[:, pl.ds(176, 16), :],
                      halo_send.at[1], halo_recv.at[1], south, lon)
    to_east = remote(pack_e, got_w, halo_send.at[2], halo_recv.at[2], lat, east)
    to_west = remote(pack_w, got_e, halo_send.at[3], halo_recv.at[3], lat, west)
    to_ne = remote(pack_e.at[pl.ds(24, 16), :], corner.at[0], halo_send.at[4], halo_recv.at[4], north, east)
    to_nw = remote(pack_w.at[pl.ds(24, 16), :], corner.at[1], halo_send.at[5], halo_recv.at[5], north, west)
    to_se = remote(pack_e.at[pl.ds(0, 16), :], corner.at[2], halo_send.at[6], halo_recv.at[6], south, east)
    to_sw = remote(pack_w.at[pl.ds(0, 16), :], corner.at[3], halo_send.at[7], halo_recv.at[7], south, west)

    to_east.start()
    to_west.start()
    next_level(0)

    @pl.when(jnp.logical_not(top))
    def _():
        to_ne.start()
        to_nw.start()
        to_north.start()

    @pl.when(jnp.logical_not(bottom))
    def _():
        to_se.start()
        to_sw.start()
        to_south.start()

    fold_z_copies = [
        remote(fold_send.at[d], fold_got.at[zi], fz_send.at[d - 1], fz_recv.at[d - 1],
               lat, ((zi + d) % NZ) * NX + xi)
        for d in range(1, NZ)
    ]
    lane32 = lanes_of((32, COLS))
    near = lane32 <= pivot_lane

    @pl.when(top)
    def _():
        next_level(1)
        next_level(2)
        for copy in fold_x_copies:
            copy.wait_recv()
        for d in far_first(NZ) + [0]:
            want = pivot_block - ((zi + d) % NZ) * NX - xi

            def block(b):
                mine = (lax.shift_right_logical(b & (LON - 1), 2) == zi)
                return fold_row[jnp.where(mine, b & (NX - 1), NX)]

            ahead, here, behind, beyond = (block(want + o) for o in (1, 0, -1, -2))
            window = jnp.where(near, here, behind)
            edge = jnp.where(
                lane32 < 9, jnp.where(near, behind, beyond),
                jnp.where(lane32 >= 119, jnp.where(near, ahead, here), 0.0),
            )
            edges = sum(pltpu.roll(edge[8 * g : 8 * g + 8], 16 + 32 * g, 1) for g in range(4))
            if d:
                fold_send[d, 0:32, :] = window
                fold_send[d, 32:40, :] = edges
                fold_z_copies[d - 1].start()
            else:
                fold_got[zi, 0:32, :] = window
                fold_got[zi, 32:40, :] = edges

    def own_strips(spans):
        for r, n in spans:
            depth, residual, search = (raw_m[f, r : r + n, :] for f in range(3))
            lane = lanes_of((n, COLS))
            west_p, east_r, west_r = (within(lane, a, a + 18) for a in (WEST, 46, WEST + 64))
            east_p = lane >= 110
            for ref, p, q in ((side_depth, depth, depth), (side_state, search, residual)):
                ref[r : r + n, :] = jnp.where(
                    east_p, p, jnp.where(west_p, shift(p, WEST), jnp.where(
                        east_r, shift(q, 64), jnp.where(west_r, shift(q, WEST + 64), 0.0))))

    def far_strips(r, n, from_e, from_w, places):
        lane = lanes_of((n, COLS))
        west_p, east_r, west_r = (within(lane, a, a + 9) for a in (WEST - 9, 64, WEST + 55))
        east_p = lane < 9
        at_d, at_r, at_p = places
        for ref, p, q in ((side_depth, at_d, at_d), (side_state, at_p, at_r)):
            ref[r : r + n, :] = jnp.where(
                east_p, shift(from_e, -p), jnp.where(west_p, shift(from_w, WEST - 9 - p), jnp.where(
                    east_r, shift(from_e, 64 - q), jnp.where(
                        west_r, shift(from_w, WEST + 55 - q), ref[r : r + n, :]))))

    kinds = {
        "m": (raw_m.at[0], s_m, de_m, se_m, w_m),
        "s": (side_depth, s_s, de_s, se_s, w_s),
    }

    def fields(kind, spans):
        for r, n in spans:
            wet = (kinds[kind][0][r : r + n, :] > 0.0).astype(F32)
            if kind == "m":
                b_m[0, r : r + n, :] = wet * raw_m[2, r : r + n, :]
                b_m[FIRST, r : r + n, :] = wet * raw_m[1, r : r + n, :]
            else:
                b_s[0, r : r + n, :] = wet * side_state[r : r + n, :]

    def roots(kind, spans):
        depth_ref_, s, de, se, _ = kinds[kind]
        for r, n in spans:
            up, depth, low = (depth_ref_[r + o : r + o + n, :] for o in (1, 0, -1))
            both = up + low
            column = depth + 0.5 * both
            wet_up, wet, wet_low = ((v > 0.0).astype(F32) for v in (up, depth, low))
            both_wet = wet_up + wet_low
            column_wet = wet + 0.5 * both_wet
            all_depth = both + (from_east(column) + from_west(column))
            all_wet = both_wet + (from_east(column_wet) + from_west(column_wet))
            total = 0.5 * (depth * all_wet + all_depth)
            diagonal = wet * (depth * (1.0 / (REACH * REACH)) + total) + (1.0 - wet)
            root = wet * lax.rsqrt(diagonal)
            s[r : r + n, :] = root
            se[r : r + n, :] = from_east(root)
            de[r : r + n, :] = from_east(depth)

    def links(kind, spans):
        depth_ref_, s, de, se, w = kinds[kind]
        for r, n in spans:
            d0, d1 = depth_ref_[r : r + n, :], depth_ref_[r + 1 : r + 1 + n, :]
            s0, s1 = s[r : r + n, :], s[r + 1 : r + 1 + n, :]
            de0, de1 = de[r : r + n, :], de[r + 1 : r + 1 + n, :]
            se0, se1 = se[r : r + n, :], se[r + 1 : r + 1 + n, :]
            east_w = -(d0 + de0) * (s0 * se0)
            ne_w = -0.5 * (d0 + de1) * (s0 * se1)
            nw_e = -0.5 * (de0 + d1) * (se0 * s1)
            w[0, r : r + n, :] = -(d0 + d1) * (s0 * s1)
            w[1, r : r + n, :] = east_w
            w[2, r : r + n, :] = from_west(east_w)
            w[3, r : r + n, :] = ne_w
            w[4, r : r + n, :] = from_west(ne_w)
            w[5, r : r + n, :] = from_west(nw_e)
            w[6, r : r + n, :] = nw_e

    def fold8(x):
        return sum(x[8 * k : 8 * k + 8] for k in range(x.shape[0] // 8))

    lane1 = lanes_of((1, COLS))
    main_lanes = within(lane1, 9, 119)
    strips_p, strips_r = strip_lanes(lane1, 0), strip_lanes(lane1, 64)

    def apply(b, k, w, r, size):
        up, mid, low = (b[k, r + o : r + o + size, :] for o in (1, 0, -1))
        a_u, a_d, e_u, e_c, e_d, f_u, f_c, f_d = w
        east_part = from_east(e_u * up + e_c * mid + e_d * low)
        west_part = from_west(f_u * up + f_c * mid + f_d * low)
        return mid, (a_u * up + a_d * low) + (east_part + west_part)

    def step(n, tasks, first, last):
        total = {}

        def add(key, product, lo, hi):
            value = fold8(product[lo:hi])
            total[key] = total[key] + value if key in total else value

        for kind, r, size, gram_lo, gram_hi in tasks:
            w = kinds[kind][4]
            weights = (
                w[0, r : r + size, :], w[0, r - 1 : r - 1 + size, :],
                w[4, r : r + size, :], w[2, r : r + size, :], w[5, r - 1 : r - 1 + size, :],
                w[6, r : r + size, :], w[1, r : r + size, :], w[3, r - 1 : r - 1 + size, :],
            )
            b, bases = (b_s, (0,)) if kind == "s" else (b_m, (0,) if last else (0, FIRST))
            news, olds = [], []
            for base in bases:
                mid, out = apply(b, base + n - 1, weights, r, size)
                out = 0.5 * out if first else out - b[base + n - 2, r : r + size, :]
                b[base + n, r : r + size, :] = out
                news.append(out)
                olds.append(mid)
            lo, hi = max(r, gram_lo) - r, min(r + size, gram_hi) - r
            if hi <= lo:
                continue
            p1, p0 = news[0], olds[0]
            if kind == "s":
                add("s0", p1 * p1, lo, hi)
                add("s1", p1 * p0, lo, hi)
                add("s4", p1 * shift(p1, 64), lo, hi)
                add("s5", p1 * shift(p0, 64), lo, hi)
                continue
            add("m0", p1 * p1, lo, hi)
            add("m1", p1 * p0, lo, hi)
            if last:
                r0 = b_m[FIRST + STEPS - 1, r : r + size, :]
            else:
                r1, r0 = news[1], olds[1]
                add("m2", r1 * r1, lo, hi)
                add("m3", r1 * r0, lo, hi)
                add("m4", p1 * r1, lo, hi)
            add("m5", p1 * r0, lo, hi)
        gather(n, total)

    def gather(n, total):
        rows = {key: jnp.sum(value, axis=0, keepdims=True) for key, value in total.items()}
        for c in range(6):
            row = jnp.zeros((1, COLS), F32)
            if "m%d" % c in rows:
                row = jnp.where(main_lanes, rows["m%d" % c], row)
            source = "s%d" % (c - 2 if c in (2, 3) else c)
            if source in rows:
                row = row + jnp.where(strips_r if c in (2, 3) else strips_p, rows[source], 0.0)
            at = pl.ds(6 * n + c, 1)
            rows_acc[at, :] = rows_acc[at, :] + row

    def steps(tasks):
        step(1, tasks, True, False)

        @pl.loop(2, STEPS)
        def _(n):
            step(n, tasks, False, False)

        step(STEPS, tasks, False, True)

    def tasks(kind, start, stop, gram_lo, gram_hi):
        return [(kind, r, n, gram_lo, gram_hi) for r, n in chunks(start, stop)]

    own_strips(chunks(16, 176))
    fields("m", chunks(16, 176))
    roots("m", [(17, 7)] + chunks(24, 168) + [(168, 7)])
    links("m", chunks(16, 168))

    @pl.when(jnp.logical_not(top))
    def _():
        next_level(1)

    start = {}
    for r, n in chunks(16, 176):
        p0, r0 = b_m[0, r : r + n, :], b_m[FIRST, r : r + n, :]
        for key, value in (("m0", p0 * p0), ("m2", r0 * r0), ("m4", p0 * r0)):
            start[key] = start[key] + fold8(value) if key in start else fold8(value)
    gather(0, start)
    steps(tasks("m", 16, 168, 32, 160))

    @pl.when(jnp.logical_not(top))
    def _():
        next_level(2)

    to_east.wait()
    to_west.wait()
    for g in range(4):
        at = 32 * g
        far_strips(16 + 40 * g, 40, got_e[...], got_w[...], (at, at + 9, at + 18))
    fields("s", chunks(16, 176))
    start = {}
    for r, n in chunks(16, 176):
        p0 = b_s[0, r : r + n, :]
        for key, value in (("s0", p0 * p0), ("s4", p0 * shift(p0, 64))):
            start[key] = start[key] + fold8(value) if key in start else fold8(value)
    gather(0, start)

    def from_south():
        @pl.when(jnp.logical_not(bottom))
        def _():
            to_se.wait_send()
            to_sw.wait_send()
            to_south.wait_send()
            to_ne.wait_recv()
            to_nw.wait_recv()
            to_north.wait_recv()
            own_strips([(0, 16)])
            far_strips(0, 16, corner[1], corner[0], (96, 105, 114))

        @pl.when(bottom)
        def _():
            for f in range(3):
                raw_m[f, 0:16, :] = jnp.zeros((16, COLS), F32)
            side_depth[0:16, :] = jnp.zeros((16, COLS), F32)
            side_state[0:16, :] = jnp.zeros((16, COLS), F32)

    @pl.when(jnp.logical_not(top))
    def _():
        from_south()
        to_ne.wait_send()
        to_nw.wait_send()
        to_north.wait_send()
        to_se.wait_recv()
        to_sw.wait_recv()
        to_south.wait_recv()
        own_strips([(176, 16)])
        far_strips(176, 16, corner[3], corner[2], (0, 9, 18))
        for kind in ("m", "s"):
            fields(kind, [(LO, 8), (176, 8)])
        roots("m", [(LO, 16), (168, 16)])
        roots("s", chunks(LO, 184))
        links("m", [(LO, 16), (168, 16)])
        links("s", chunks(LO, 184))
        steps([("m", LO, 24, 16, 32), ("m", 160, 24, 160, 176)] + tasks("s", LO, 184, 16, 176))

    @pl.when(top)
    def _():
        from_south()
        for kind in ("m", "s"):
            fields(kind, [(LO, 8)])
        roots("m", [(LO, 16)])
        roots("s", chunks(LO, 168) + [(168, 7)])
        links("m", [(LO, 16)])
        links("s", chunks(LO, 168))
        steps([("m", LO, 24, 16, 32)] + tasks("s", LO, 168, 16, 160))
        for copy in fold_z_copies:
            copy.wait_recv()
        ghost = fold_got[0]
        for k in range(1, NZ):
            ghost = ghost + fold_got[k]
        edges = ghost[32:40]
        lane8 = lanes_of((8, COLS))
        side = []
        for g in range(4):
            edge = pltpu.roll(edges, (COLS - 16 - 32 * g) % COLS, 1)
            side.append(jnp.where((lane8 < 9) | (lane8 >= 119), edge, 0.0))
        side = jnp.concatenate(side, axis=0)
        for f in range(3):
            raw_m[f, 176:192, :] = jnp.zeros((16, COLS), F32)
        raw_m[0, 176:185, :] = ghost[0:9]
        raw_m[1, 176:184, :] = ghost[9:17]
        raw_m[2, 176:184, :] = ghost[17:25]
        own_strips([(176, 16)])
        fold_x[...] = side
        west_p, west_r, east_r = (within(lane1, a, a + 9) for a in (WEST - 9, WEST + 55, 64))
        for ref, p, q, count in ((side_depth, 0, 0, 9), (side_state, 17, 9, 8)):
            one, two = fold_x[p : p + count, :], fold_x[q : q + count, :]
            ref[176 : 176 + count, :] = jnp.where(
                lane1 < 9, one, jnp.where(west_p, shift(one, WEST), jnp.where(
                    east_r, shift(two, 64), jnp.where(
                        west_r, shift(two, WEST + 64), ref[176 : 176 + count, :]))))
        for kind in ("m", "s"):
            fields(kind, [(176, 8)])
            roots(kind, [(168, 16)])
            links(kind, [(168, 16)])
        steps([("m", 160, 24, 160, 176), ("s", 160, 24, 160, 176)])
        for copy in fold_x_copies + fold_z_copies:
            copy.wait_send()

    ones = jnp.ones((8, COLS), F32)
    sums = lax.dot_general(
        ones, rows_acc[...], (((1,), (1,)), ((), ())), precision=HIGHEST, preferred_element_type=F32
    )[0:1]

    def reduce(stage, value, slots, send, recv, count, mine, peer_of, order):
        slots[mine] = value
        part[stage] = value
        copies = [
            remote(part.at[stage], slots.at[mine], send.at[d - 1], recv.at[d - 1], *peer_of(d))
            for d in range(1, count)
        ]
        for d in order:
            copies[d - 1].start()
        for copy in copies:
            copy.wait_recv()
        terms = [slots[k] for k in range(count)]
        while len(terms) > 1:
            terms = [a + b for a, b in zip(terms[::2], terms[1::2])]
        return terms[0], copies

    sums, first_copies = reduce(
        0, sums, red_y, ry_send, ry_recv, LAT, lat,
        lambda d: ((lat + d) % LAT, lon), far_first(LAT))
    next_level(levels)
    sums, second_copies = reduce(
        1, sums, red_p, rp_send, rp_recv, LON, lon,
        lambda d: (lat, (lon + d) % LON), far_first(LON))
    moments_out[...] = sums
    for copy in first_copies + second_copies:
        copy.wait_send()


def held(shape):
    return pltpu.VMEM(shape, F32)


def basis_and_moments(forcing, search, depth, mask, fold_map):
    vm = pltpu.VMEM
    dma = pltpu.SemaphoreType.DMA
    ext = (EXT, COLS)
    return pl.pallas_call(
        basis_kernel,
        out_shape=(held((FIELDS,) + ext), held((STEPS + 1,) + ext), held((1, COLS))),
        in_specs=[pl.BlockSpec(memory_space=pl.ANY)] * 5,
        out_specs=(pl.BlockSpec(memory_space=vm),) * 3,
        scratch_shapes=[
            pltpu.SMEM((1024,), jnp.int32),
            vm((3,) + ext, F32), vm(ext, F32), vm(ext, F32),
            vm((ROWS, COLS), F32), vm((ROWS, COLS), jnp.int32),
            vm((40, COLS), F32), vm((40, COLS), F32), vm((40, COLS), F32), vm((40, COLS), F32),
            vm((4, 16, COLS), F32),
            vm((32, COLS), F32), vm((32, COLS), F32), vm((NX + 1, 32, COLS), F32),
            vm((NZ, 40, COLS), F32), vm((NZ, 40, COLS), F32),
        ]
        + [vm(ext, F32)] * 6
        + [vm((7,) + ext, F32)] * 2
        + [
            vm((COLS, COLS), F32), vm((2, 1, COLS), F32),
            vm((LON, 1, COLS), F32), vm((LAT, 1, COLS), F32),
            pltpu.SemaphoreType.REGULAR((4,)), dma((5,)), dma((8,)), dma((8,)),
            dma((NZ - 1,)), dma((NZ - 1,)), dma((NX - 1,)), dma((NX - 1,)),
            dma((LON - 1,)), dma((LON - 1,)), dma((LAT - 1,)), dma((LAT - 1,)),
        ],
        compiler_params=pltpu.CompilerParams(collective_id=0, has_side_effects=True),
        name="basis",
    )(fold_map, forcing, search, depth, mask)


def combine_kernel(moments_ref, basis_ref, strips_ref, height_ref, residual_ref):
    shape = (24, COLS)
    row = lax.broadcasted_iota(jnp.int32, shape, 0)
    col = lanes_of(shape)

    def power(i):
        return jnp.where(i >= FIRST, i - FIRST, i)

    kind = jnp.where((row >= FIRST) & (col >= FIRST), 1, jnp.where((row >= FIRST) | (col >= FIRST), 2, 0))
    valid = (row < FIELDS) & (col < FIELDS)
    ka, kb = power(row), power(col)
    high, low = ka + kb, jnp.abs(ka - kb)
    odd = high & 1

    def slot(k):
        return jnp.where(valid, 6 * ((k + 1) >> 1) + 2 * kind + odd, 0)

    base = jnp.where(odd == 1, 7 + 2 * kind, 2 * kind)
    raw = jnp.broadcast_to(moments_ref[...], shape)

    def take(index):
        return jnp.take_along_axis(raw, index, axis=1)

    gram = jnp.where(valid, take(slot(high)) + take(slot(low)) - take(jnp.where(valid, base, 0)), 0.0)

    def lower(i):
        return jnp.where((i == 1) | (i == FIRST + 1), 1.0, jnp.where((i >= 1) & (i < FIELDS) & (i != FIRST), 0.5, 0.0))

    def upper(i):
        return jnp.where((i < FIELDS - 2) & (i != FIRST - 2) & (i != FIRST - 1), 0.5, 0.0)

    low_l, up_l = lower(col).astype(F32), upper(col).astype(F32)
    low_s, up_s = lower(row).astype(F32), upper(row).astype(F32)

    def shifted(v, axis):
        length = v.shape[axis]
        low_c, up_c = (low_s, up_s) if axis == 0 else (low_l, up_l)
        return v + low_c * pltpu.roll(v, 1, axis) + up_c * pltpu.roll(v, length - 1, axis)

    below = pltpu.roll(low_l, COLS - 1, 1)
    above = pltpu.roll(up_l, 1, 1)
    ends = (col == FIRST - 1) | (col == FIELDS - 1)
    gram_h = jnp.where(
        ends, 0.0,
        gram + below * pltpu.roll(gram, COLS - 1, 1) + jnp.where(col > 0, above, 0.0) * pltpu.roll(gram, 1, 1),
    )

    def form(matrix, left, right):
        return jnp.sum(matrix * left * right, keepdims=True)

    unit = lambda at: ((row == at).astype(F32), (col == at).astype(F32))
    p_s, p_l = unit(0)
    r_s, r_l = unit(FIRST)
    q_s, q_l = shifted(p_s, 0), shifted(p_l, 1)
    x_s = jnp.zeros(shape, F32)
    norm = form(gram, r_s, r_l)
    curvature = form(gram_h, p_s, p_l)
    for inner in range(STEPS):
        t = norm / curvature
        x_s = x_s + t * p_s
        r_s = r_s - t * q_s
        if inner == STEPS - 1:
            break
        r_l = r_l - t * q_l
        h_s, h_l = shifted(r_s, 0), shifted(r_l, 1)
        fresh = form(gram, r_s, r_l)
        own = form(gram_h, r_s, r_l)
        cross = form(gram_h, r_s, p_l)
        beta = fresh / norm
        curvature = own + beta * (2.0 * cross + beta * curvature)
        norm = fresh
        p_s, p_l = r_s + beta * p_s, r_l + beta * p_l
        q_s, q_l = h_s + beta * q_s, h_l + beta * q_l

    lane1 = lanes_of((1, COLS))
    search_half = within((lane1 + 32) & (COLS - 1), 14, 78)
    size = 32
    for coords, out_ref in ((x_s, height_ref), (r_s, residual_ref)):
        mixed = []
        for n in range(STEPS + 1):
            other = coords[FIRST + n : FIRST + n + 1, :] if n < STEPS else jnp.zeros((1, COLS), F32)
            mixed.append(jnp.where(search_half, coords[n : n + 1, :], other))
        for at in range(0, ROWS, size):
            rows = slice(16 + at, 16 + at + size)
            main = sum(coords[k : k + 1, :] * basis_ref[k, rows, :] for k in range(FIELDS))
            strip = sum(mixed[n] * strips_ref[n, rows, :] for n in range(STEPS + 1))
            strip = strip + shift(strip, 64)
            out_ref[at : at + size, :] = jnp.where(
                lane1 >= 119, strip, jnp.where(lane1 < 9, shift(strip, -WEST), main)
            )


def per_device(forcing, search, depth, mask, fold_map):
    made = basis_and_moments(forcing, search, depth, mask, fold_map)
    basis, strips, moments = (pltpu.with_memory_space_constraint(v, pltpu.VMEM) for v in made)
    block = jax.ShapeDtypeStruct((ROWS, COLS), F32)
    return pl.pallas_call(
        combine_kernel,
        out_shape=(block, block),
        in_specs=[pl.BlockSpec(memory_space=pltpu.VMEM)] * 3,
        name="combine",
    )(moments, basis, strips)


def solution(mesh):
    return jax.shard_map(
        per_device,
        mesh=mesh,
        in_specs=(P("lat", "lon"),) * 4 + (P(),),
        out_specs=(P("lat", "lon"),) * 2,
        check_vma=False,
    )
```

time: 37.6 us -> 37.1 us (0.987)
  Pallas kernels: 36.8 us -> 36.3 us
    pallas_call x1, Pallas kernels: 34.7 us -> 34.1 us  [basis_and_moments(): pl.pallas_call(basis_kernel, out_shape=(held((FIELDS,) + ext), held((STEP...]
where the time goes in v4:
time: 37.1 us; the launch traced here: 36.9 us
  Pallas kernels  36.3 us (98%)
  between operations  0.64 us (2%)
    pallas_call x1, Pallas kernels, basis_and_moments(): pl.pallas_call(basis_kernel, out_shape=(held((FIELDS,) + ext), held((STEP...  34.1 us
    pallas_call x1, Pallas kernels, per_device(): pl.pallas_call(combine_kernel, out_shape=(block, block), in_specs=[pl.Blo...  2.18 us

profile of v4, /device:TPU:1, one launch (start us, length us, event | category | flops | bytes accessed | tf_op | source)
XLA Modules:
  0.0 36.9 jit_solution(15791506183100092989)
XLA Ops:
  0.6 34.1 %basis.1 = (f32[17,192,128]{2,1,0:T(8,128)S(1)}, f32[9,192,128]{2,1,0:T(8,128)S(1)}, f32[1,128]{1,0:T(1,128)S(1)}) custom-call(s32[4096]{0:T(1024)} %fold_ref.1, f32[160,128]{1,0:T(8,128)} %forcing_ref.1, f32[160,128]{1,0:T(8,128)} %search_ref.1, f32[160,128]{1,0:T(8,128)} %depth_ref.1, s32[160,128]{1,0:T(8,128)} %mask_ref.1), custom_call_target="tpu_custom_call" | custom-call | tf_op jit(solution)/shard_map/basis/pallas_call | solution.py:553
  34.7 2.2 %combine.1 = (f32[160,128]{1,0:T(8,128)}, f32[160,128]{1,0:T(8,128)}) custom-call(f32[1,128]{1,0:T(1,128)S(1)} %get-tuple-element.5.moments_ref, f32[17,192,128]{2,1,0:T(8,128)S(1)} %get-tuple-element.6.basis_ref, f32[9,192,128]{2,1,0:T(8,128)S(1)} %get-tuple-element.7.strips_ref), custom_call_target="tpu_custom_call" | custom-call | tf_op jit(solution)/shard_map/combine/pallas_call | solution.py:677

commit v5 on v4

--- a/solution.py
+++ b/solution.py
@@ -83,6 +83,7 @@
     lat = lax.axis_index("lat")
     lon = lax.axis_index("lon")
     zi, xi = lon // NX, lon % NX
+    core, yi = lat % 2, lat // 2
     top = lat == LAT - 1
     bottom = lat == 0
     north, south = (lat + 1) % LAT, (lat + LAT - 1) % LAT
@@ -117,6 +118,7 @@
     beside += [(north, east), (north, west), (south, east), (south, west)]
     beside += [(lat, east), (lat, west), (north, lon), (south, lon)] + around(1)
 
+    beside += [(lat + 1 - 2 * core, zi * NX + (xi + d) % NX) for d in far_first(NX)]
     greet(barrier, beside)
 
     levels = 3
@@ -131,19 +133,6 @@
     for copy in loads:
         copy.wait()
     raw_m[0, 16 : 16 + ROWS, :] = depth_buf[...] * mask_buf[...].astype(F32)
-
-    lane40 = lanes_of((40, COLS))
-    acc_w = jnp.zeros((40, COLS), F32)
-    acc_e = jnp.zeros((40, COLS), F32)
-    for g in range(4):
-        for f in range(3):
-            at = 32 * g + 9 * f
-            block = raw_m[f, 16 + 40 * g : 56 + 40 * g, :]
-            here = (lane40 >= at) & (lane40 < at + 9)
-            acc_w = jnp.where(here, pltpu.roll(block, at, 1) if at else block, acc_w)
-            acc_e = jnp.where(here, pltpu.roll(block, (at - 119) % COLS, 1), acc_e)
-    pack_w[...] = acc_w
-    pack_e[...] = acc_e
 
     pivot = fold_buf[0]
     pivot_block, pivot_lane = lax.shift_right_logical(pivot, 7), pivot & (COLS - 1)
@@ -164,6 +153,19 @@
         fold_row[xi] = turned
         fold_row[NX] = jnp.zeros_like(turned)
 
+    lane40 = lanes_of((40, COLS))
+    acc_w = jnp.zeros((40, COLS), F32)
+    acc_e = jnp.zeros((40, COLS), F32)
+    for g in range(4):
+        for f in range(3):
+            at = 32 * g + 9 * f
+            block = raw_m[f, 16 + 40 * g : 56 + 40 * g, :]
+            here = (lane40 >= at) & (lane40 < at + 9)
+            acc_w = jnp.where(here, pltpu.roll(block, at, 1) if at else block, acc_w)
+            acc_e = jnp.where(here, pltpu.roll(block, (at - 119) % COLS, 1), acc_e)
+    pack_w[...] = acc_w
+    pack_e[...] = acc_e
+
     pl.semaphore_wait(barrier, len(beside))
 
     fold_x_copies = [
@@ -234,10 +236,11 @@
             if d:
                 fold_send[d, 0:32, :] = window
                 fold_send[d, 32:40, :] = edges
-                fold_z_copies[d - 1].start()
             else:
                 fold_got[zi, 0:32, :] = window
                 fold_got[zi, 32:40, :] = edges
+        for d in far_first(NZ):
+            fold_z_copies[d - 1].start()
 
     def own_strips(spans):
         for r, n in spans:
@@ -514,31 +517,64 @@
         ones, rows_acc[...], (((1,), (1,)), ((), ())), precision=HIGHEST, preferred_element_type=F32
     )[0:1]
 
-    def reduce(stage, value, slots, send, recv, count, mine, peer_of, order):
-        slots[mine] = value
-        part[stage] = value
-        copies = [
-            remote(part.at[stage], slots.at[mine], send.at[d - 1], recv.at[d - 1], *peer_of(d))
-            for d in range(1, count)
-        ]
-        for d in order:
-            copies[d - 1].start()
-        for copy in copies:
-            copy.wait_recv()
-        terms = [slots[k] for k in range(count)]
+    def tree(terms):
         while len(terms) > 1:
             terms = [a + b for a, b in zip(terms[::2], terms[1::2])]
-        return terms[0], copies
-
-    sums, first_copies = reduce(
-        0, sums, red_y, ry_send, ry_recv, LAT, lat,
-        lambda d: ((lat + d) % LAT, lon), far_first(LAT))
+        return terms[0]
+
+    second = core == 1
+    part[0] = sums
     next_level(levels)
-    sums, second_copies = reduce(
-        1, sums, red_p, rp_send, rp_recv, LON, lon,
-        lambda d: (lat, (lon + d) % LON), far_first(LON))
-    moments_out[...] = sums
-    for copy in first_copies + second_copies:
+    to_plane = [
+        remote(part.at[0], red_p.at[core * LON + lon], rp_send.at[d], rp_recv.at[core * LON + d],
+               2 * yi + 1, (lon + d) % LON)
+        for d in range(LON)
+    ]
+    for d in far_first(LON):
+        to_plane[d].start()
+    count = LAT // 2
+    along_y = [(d, c) for d in far_first(count) + [0] for c in (1, 0) if (d, c) != (0, 1)]
+    to_lat = [
+        remote(part.at[1], red_y.at[yi], ry_send.at[2 * d + c], ry_recv.at[d],
+               2 * ((yi + d) % count) + c, lon)
+        for d, c in along_y
+    ]
+
+    @pl.when(jnp.logical_not(second))
+    def _():
+        to_plane[0].start()
+        to_plane[0].wait_send()
+
+    @pl.when(second)
+    def _():
+        red_p[LON + lon] = sums
+        for c in range(2):
+            for d in range(c, LON):
+                remote(part.at[0], red_p.at[c * LON + lon], rp_send.at[d], rp_recv.at[c * LON + d],
+                       lat, east).wait_recv()
+        total = tree([red_p[k] for k in range(2 * LON)])
+        part[1] = total
+        red_y[yi] = total
+        for copy in to_lat:
+            copy.start()
+
+    def arrived(d):
+        remote(part.at[1], red_y.at[yi], ry_send.at[0], ry_recv.at[d], lat, east).wait_recv()
+
+    @pl.when(jnp.logical_not(second))
+    def _():
+        arrived(0)
+
+    for d in range(1, count):
+        arrived(d)
+    moments_out[...] = tree([red_y[k] for k in range(count)])
+
+    @pl.when(second)
+    def _():
+        for copy in to_lat:
+            copy.wait_send()
+
+    for copy in to_plane[1:]:
         copy.wait_send()
 
 
@@ -568,10 +604,10 @@
         + [vm((7,) + ext, F32)] * 2
         + [
             vm((COLS, COLS), F32), vm((2, 1, COLS), F32),
-            vm((LON, 1, COLS), F32), vm((LAT, 1, COLS), F32),
+            vm((2 * LON, 1, COLS), F32), vm((LAT // 2, 1, COLS), F32),
             pltpu.SemaphoreType.REGULAR((4,)), dma((5,)), dma((8,)), dma((8,)),
             dma((NZ - 1,)), dma((NZ - 1,)), dma((NX - 1,)), dma((NX - 1,)),
-            dma((LON - 1,)), dma((LON - 1,)), dma((LAT - 1,)), dma((LAT - 1,)),
+            dma((LON,)), dma((2 * LON,)), dma((LAT,)), dma((LAT // 2,)),
         ],
         compiler_params=pltpu.CompilerParams(collective_id=0, has_side_effects=True),
         name="basis",

time: 37.1 us -> 37.3 us (level)
  no operation moved by 1% of the time
where the time goes in v5:
time: 37.3 us; the launch traced here: 37.1 us
  Pallas kernels  36.5 us (98%)
  between operations  0.64 us (2%)
    pallas_call x1, Pallas kernels, basis_and_moments(): pl.pallas_call(basis_kernel, out_shape=(held((FIELDS,) + ext), held((STEP...  34.3 us
    pallas_call x1, Pallas kernels, per_device(): pl.pallas_call(combine_kernel, out_shape=(block, block), in_specs=[pl.Blo...  2.18 us

profile of v5, /device:TPU:1, one launch (start us, length us, event | category | flops | bytes accessed | tf_op | source)
XLA Modules:
  0.0 37.1 jit_solution(16175632140118996858)
XLA Ops:
  0.6 34.3 %basis.1 = (f32[17,192,128]{2,1,0:T(8,128)S(1)}, f32[9,192,128]{2,1,0:T(8,128)S(1)}, f32[1,128]{1,0:T(1,128)S(1)}) custom-call(s32[4096]{0:T(1024)} %fold_ref.1, f32[160,128]{1,0:T(8,128)} %forcing_ref.1, f32[160,128]{1,0:T(8,128)} %search_ref.1, f32[160,128]{1,0:T(8,128)} %depth_ref.1, s32[160,128]{1,0:T(8,128)} %mask_ref.1), custom_call_target="tpu_custom_call" | custom-call | tf_op jit(solution)/shard_map/basis/pallas_call | solution.py:589
  34.9 2.2 %combine.1 = (f32[160,128]{1,0:T(8,128)}, f32[160,128]{1,0:T(8,128)}) custom-call(f32[1,128]{1,0:T(1,128)S(1)} %get-tuple-element.5.moments_ref, f32[17,192,128]{2,1,0:T(8,128)S(1)} %get-tuple-element.6.basis_ref, f32[9,192,128]{2,1,0:T(8,128)S(1)} %get-tuple-element.7.strips_ref), custom_call_target="tpu_custom_call" | custom-call | tf_op jit(solution)/shard_map/combine/pallas_call | solution.py:713

commit v6 on v5

--- a/solution.py
+++ b/solution.py
@@ -411,11 +411,12 @@
         for key, value in (("m0", p0 * p0), ("m2", r0 * r0), ("m4", p0 * r0)):
             start[key] = start[key] + fold8(value) if key in start else fold8(value)
     gather(0, start)
+
+    @pl.when(jnp.logical_not(top))
+    def _():
+        next_level(2)
+
     steps(tasks("m", 16, 168, 32, 160))
-
-    @pl.when(jnp.logical_not(top))
-    def _():
-        next_level(2)
 
     to_east.wait()
     to_west.wait()
@@ -430,28 +431,30 @@
             start[key] = start[key] + fold8(value) if key in start else fold8(value)
     gather(0, start)
 
-    def from_south():
-        @pl.when(jnp.logical_not(bottom))
-        def _():
-            to_se.wait_send()
-            to_sw.wait_send()
-            to_south.wait_send()
-            to_ne.wait_recv()
-            to_nw.wait_recv()
-            to_north.wait_recv()
-            own_strips([(0, 16)])
-            far_strips(0, 16, corner[1], corner[0], (96, 105, 114))
-
-        @pl.when(bottom)
-        def _():
-            for f in range(3):
-                raw_m[f, 0:16, :] = jnp.zeros((16, COLS), F32)
-            side_depth[0:16, :] = jnp.zeros((16, COLS), F32)
-            side_state[0:16, :] = jnp.zeros((16, COLS), F32)
+    roots("s", [(17, 7)] + chunks(24, 168) + [(168, 7)])
+    links("s", chunks(16, 168))
+    steps(tasks("s", 16, 168, 32, 160))
+
+    @pl.when(jnp.logical_not(bottom))
+    def _():
+        to_se.wait_send()
+        to_sw.wait_send()
+        to_south.wait_send()
+        to_ne.wait_recv()
+        to_nw.wait_recv()
+        to_north.wait_recv()
+        own_strips([(0, 16)])
+        far_strips(0, 16, corner[1], corner[0], (96, 105, 114))
+
+    @pl.when(bottom)
+    def _():
+        for f in range(3):
+            raw_m[f, 0:16, :] = jnp.zeros((16, COLS), F32)
+        side_depth[0:16, :] = jnp.zeros((16, COLS), F32)
+        side_state[0:16, :] = jnp.zeros((16, COLS), F32)
 
     @pl.when(jnp.logical_not(top))
     def _():
-        from_south()
         to_ne.wait_send()
         to_nw.wait_send()
         to_north.wait_send()
@@ -460,24 +463,9 @@
         to_south.wait_recv()
         own_strips([(176, 16)])
         far_strips(176, 16, corner[3], corner[2], (0, 9, 18))
-        for kind in ("m", "s"):
-            fields(kind, [(LO, 8), (176, 8)])
-        roots("m", [(LO, 16), (168, 16)])
-        roots("s", chunks(LO, 184))
-        links("m", [(LO, 16), (168, 16)])
-        links("s", chunks(LO, 184))
-        steps([("m", LO, 24, 16, 32), ("m", 160, 24, 160, 176)] + tasks("s", LO, 184, 16, 176))
 
     @pl.when(top)
     def _():
-        from_south()
-        for kind in ("m", "s"):
-            fields(kind, [(LO, 8)])
-        roots("m", [(LO, 16)])
-        roots("s", chunks(LO, 168) + [(168, 7)])
-        links("m", [(LO, 16)])
-        links("s", chunks(LO, 168))
-        steps([("m", LO, 24, 16, 32)] + tasks("s", LO, 168, 16, 160))
         for copy in fold_z_copies:
             copy.wait_recv()
         ghost = fold_got[0]
@@ -504,13 +492,14 @@
                 lane1 < 9, one, jnp.where(west_p, shift(one, WEST), jnp.where(
                     east_r, shift(two, 64), jnp.where(
                         west_r, shift(two, WEST + 64), ref[176 : 176 + count, :]))))
-        for kind in ("m", "s"):
-            fields(kind, [(176, 8)])
-            roots(kind, [(168, 16)])
-            links(kind, [(168, 16)])
-        steps([("m", 160, 24, 160, 176), ("s", 160, 24, 160, 176)])
         for copy in fold_x_copies + fold_z_copies:
             copy.wait_send()
+
+    for kind in ("m", "s"):
+        fields(kind, [(LO, 8), (176, 8)])
+        roots(kind, [(LO, 16), (168, 16)])
+        links(kind, [(LO, 16), (168, 16)])
+    steps([(kind, r, 24, lo, lo + 16) for kind in ("m", "s") for r, lo in ((LO, 16), (160, 160))])
 
     ones = jnp.ones((8, COLS), F32)
     sums = lax.dot_general(

time: 37.3 us -> 37.2 us (level)
  no operation moved by 1% of the time
where the time goes in v6:
time: 37.2 us; the launch traced here: 37.1 us
  Pallas kernels  36.4 us (98%)
  between operations  0.64 us (2%)
    pallas_call x1, Pallas kernels, basis_and_moments(): pl.pallas_call(basis_kernel, out_shape=(held((FIELDS,) + ext), held((STEP...  34.3 us
    pallas_call x1, Pallas kernels, per_device(): pl.pallas_call(combine_kernel, out_shape=(block, block), in_specs=[pl.Blo...  2.18 us

profile of v6, /device:TPU:1, one launch (start us, length us, event | category | flops | bytes accessed | tf_op | source)
XLA Modules:
  0.0 37.1 jit_solution(4192948200697632028)
XLA Ops:
  0.6 34.3 %basis.1 = (f32[17,192,128]{2,1,0:T(8,128)S(1)}, f32[9,192,128]{2,1,0:T(8,128)S(1)}, f32[1,128]{1,0:T(1,128)S(1)}) custom-call(s32[4096]{0:T(1024)} %fold_ref.1, f32[160,128]{1,0:T(8,128)} %forcing_ref.1, f32[160,128]{1,0:T(8,128)} %search_ref.1, f32[160,128]{1,0:T(8,128)} %depth_ref.1, s32[160,128]{1,0:T(8,128)} %mask_ref.1), custom_call_target="tpu_custom_call" | custom-call | tf_op jit(solution)/shard_map/basis/pallas_call | solution.py:578
  34.9 2.2 %combine.1 = (f32[160,128]{1,0:T(8,128)}, f32[160,128]{1,0:T(8,128)}) custom-call(f32[1,128]{1,0:T(1,128)S(1)} %get-tuple-element.5.moments_ref, f32[17,192,128]{2,1,0:T(8,128)S(1)} %get-tuple-element.6.basis_ref, f32[9,192,128]{2,1,0:T(8,128)S(1)} %get-tuple-element.7.strips_ref), custom_call_target="tpu_custom_call" | custom-call | tf_op jit(solution)/shard_map/combine/pallas_call | solution.py:702

commit v7 on v6

--- a/solution.py
+++ b/solution.py
@@ -603,91 +603,85 @@
     )(fold_map, forcing, search, depth, mask)
 
 
-def combine_kernel(moments_ref, basis_ref, strips_ref, height_ref, residual_ref):
-    shape = (24, COLS)
-    row = lax.broadcasted_iota(jnp.int32, shape, 0)
-    col = lanes_of(shape)
-
-    def power(i):
-        return jnp.where(i >= FIRST, i - FIRST, i)
-
-    kind = jnp.where((row >= FIRST) & (col >= FIRST), 1, jnp.where((row >= FIRST) | (col >= FIRST), 2, 0))
-    valid = (row < FIELDS) & (col < FIELDS)
-    ka, kb = power(row), power(col)
-    high, low = ka + kb, jnp.abs(ka - kb)
-    odd = high & 1
-
-    def slot(k):
-        return jnp.where(valid, 6 * ((k + 1) >> 1) + 2 * kind + odd, 0)
-
+def rows_of(shape):
+    return lax.broadcasted_iota(jnp.int32, shape, 0)
+
+
+def applied_to_coords(c):
+    row = rows_of(c.shape)
+    below = jnp.where(row == 0, 0.0, jnp.where(row == 1, 1.0, 0.5)).astype(F32)
+    above = jnp.where(row == c.shape[0] - 1, 0.0, 0.5).astype(F32)
+    return c + below * pltpu.roll(c, 1, 0) + above * pltpu.roll(c, c.shape[0] - 1, 0)
+
+
+def applied_to_moments(m):
+    row = rows_of(m.shape)
+    up, down = pltpu.roll(m, m.shape[0] - 1, 0), pltpu.roll(m, 1, 0)
+    return m + 0.5 * (up + jnp.where(row == 0, up, down))
+
+
+def moment_rows(raw, kind, count):
+    k = rows_of((count, COLS))
+    odd = k & 1
+    high = jnp.minimum(6 * ((k + 1) >> 1) + 2 * kind + odd, COLS - 1)
+    spread = jnp.broadcast_to(raw, (count, COLS))
     base = jnp.where(odd == 1, 7 + 2 * kind, 2 * kind)
-    raw = jnp.broadcast_to(moments_ref[...], shape)
-
-    def take(index):
-        return jnp.take_along_axis(raw, index, axis=1)
-
-    gram = jnp.where(valid, take(slot(high)) + take(slot(low)) - take(jnp.where(valid, base, 0)), 0.0)
-
-    def lower(i):
-        return jnp.where((i == 1) | (i == FIRST + 1), 1.0, jnp.where((i >= 1) & (i < FIELDS) & (i != FIRST), 0.5, 0.0))
-
-    def upper(i):
-        return jnp.where((i < FIELDS - 2) & (i != FIRST - 2) & (i != FIRST - 1), 0.5, 0.0)
-
-    low_l, up_l = lower(col).astype(F32), upper(col).astype(F32)
-    low_s, up_s = lower(row).astype(F32), upper(row).astype(F32)
-
-    def shifted(v, axis):
-        length = v.shape[axis]
-        low_c, up_c = (low_s, up_s) if axis == 0 else (low_l, up_l)
-        return v + low_c * pltpu.roll(v, 1, axis) + up_c * pltpu.roll(v, length - 1, axis)
-
-    below = pltpu.roll(low_l, COLS - 1, 1)
-    above = pltpu.roll(up_l, 1, 1)
-    ends = (col == FIRST - 1) | (col == FIELDS - 1)
-    gram_h = jnp.where(
-        ends, 0.0,
-        gram + below * pltpu.roll(gram, COLS - 1, 1) + jnp.where(col > 0, above, 0.0) * pltpu.roll(gram, 1, 1),
-    )
-
-    def form(matrix, left, right):
-        return jnp.sum(matrix * left * right, keepdims=True)
-
-    unit = lambda at: ((row == at).astype(F32), (col == at).astype(F32))
-    p_s, p_l = unit(0)
-    r_s, r_l = unit(FIRST)
-    q_s, q_l = shifted(p_s, 0), shifted(p_l, 1)
-    x_s = jnp.zeros(shape, F32)
-    norm = form(gram, r_s, r_l)
-    curvature = form(gram_h, p_s, p_l)
+    return 2.0 * jnp.take_along_axis(spread, high, axis=1) - jnp.take_along_axis(spread, base, axis=1)
+
+
+def dot_rows(coords, moments):
+    (cp, cr), (mp, mr) = coords, moments
+    products = cp * mp[0:16]
+    return jnp.sum(products[0:8] + products[8:16] + cr * mr[0:8], axis=0, keepdims=True)
+
+
+def pair(function, one, two):
+    return tuple(function(a, b) for a, b in zip(one, two))
+
+
+def coordinates(raw):
+    search_search = moment_rows(raw, 0, 24)
+    residual_residual = moment_rows(raw, 1, 16)
+    mixed_long, mixed = moment_rows(raw, 2, 24), moment_rows(raw, 2, 16)
+    first16 = (rows_of((16, COLS)) == 0).astype(F32)
+    first8 = (rows_of((8, COLS)) == 0).astype(F32)
+    p, pm = (first16, jnp.zeros((8, COLS), F32)), (search_search, mixed)
+    r, rm = (jnp.zeros((16, COLS), F32), first8), (mixed_long, residual_residual)
+    x = (jnp.zeros((16, COLS), F32), jnp.zeros((8, COLS), F32))
+    q, qm = tuple(map(applied_to_coords, p)), tuple(map(applied_to_moments, pm))
+    norm, curvature = dot_rows(r, rm), dot_rows(p, qm)
     for inner in range(STEPS):
         t = norm / curvature
-        x_s = x_s + t * p_s
-        r_s = r_s - t * q_s
+        x = pair(lambda a, b: a + t * b, x, p)
+        r = pair(lambda a, b: a - t * b, r, q)
         if inner == STEPS - 1:
             break
-        r_l = r_l - t * q_l
-        h_s, h_l = shifted(r_s, 0), shifted(r_l, 1)
-        fresh = form(gram, r_s, r_l)
-        own = form(gram_h, r_s, r_l)
-        cross = form(gram_h, r_s, p_l)
+        rm = pair(lambda a, b: a - t * b, rm, qm)
+        am = tuple(map(applied_to_moments, rm))
+        fresh, own, cross = dot_rows(r, rm), dot_rows(r, am), dot_rows(p, am)
         beta = fresh / norm
         curvature = own + beta * (2.0 * cross + beta * curvature)
         norm = fresh
-        p_s, p_l = r_s + beta * p_s, r_l + beta * p_l
-        q_s, q_l = h_s + beta * q_s, h_l + beta * q_l
-
+        p = pair(lambda a, b: a + beta * b, r, p)
+        q = tuple(map(applied_to_coords, p))
+        qm = pair(lambda a, b: a + beta * b, am, qm)
+    return x, r
+
+
+def combine_kernel(moments_ref, basis_ref, strips_ref, height_ref, residual_ref):
+    found = coordinates(moments_ref[...])
     lane1 = lanes_of((1, COLS))
     search_half = within((lane1 + 32) & (COLS - 1), 14, 78)
     size = 32
-    for coords, out_ref in ((x_s, height_ref), (r_s, residual_ref)):
+    for (of_p, of_r), out_ref in zip(found, (height_ref, residual_ref)):
+        coords = [of_p[k : k + 1, :] for k in range(FIRST)] + [of_r[k : k + 1, :] for k in range(STEPS)]
         mixed = []
         for n in range(STEPS + 1):
-            other = coords[FIRST + n : FIRST + n + 1, :] if n < STEPS else jnp.zeros((1, COLS), F32)
-            mixed.append(jnp.where(search_half, coords[n : n + 1, :], other))
+            other = coords[FIRST + n] if n < STEPS else jnp.zeros((1, COLS), F32)
+            mixed.append(jnp.where(search_half, coords[n], other))
         for at in range(0, ROWS, size):
             rows = slice(16 + at, 16 + at + size)
-            main = sum(coords[k : k + 1, :] * basis_ref[k, rows, :] for k in range(FIELDS))
+            main = sum(coords[k] * basis_ref[k, rows, :] for k in range(FIELDS))
             strip = sum(mixed[n] * strips_ref[n, rows, :] for n in range(STEPS + 1))
             strip = strip + shift(strip, 64)
             out_ref[at : at + size, :] = jnp.where(

time: 37.2 us -> 36.3 us (0.976)
  Pallas kernels: 36.4 us -> 35.5 us
    pallas_call x1, Pallas kernels: 2.18 us -> 1.26 us  [per_device(): pl.pallas_call(combine_kernel, out_shape=(block, block), in_specs=[pl.Blo...]
where the time goes in v7:
time: 36.3 us; the launch traced here: 36.2 us
  Pallas kernels  35.5 us (98%)
  between operations  0.64 us (2%)
    pallas_call x1, Pallas kernels, basis_and_moments(): pl.pallas_call(basis_kernel, out_shape=(held((FIELDS,) + ext), held((STEP...  34.3 us
    pallas_call x1, Pallas kernels, per_device(): pl.pallas_call(combine_kernel, out_shape=(block, block), in_specs=[pl.Blo...  1.26 us

profile of v7, /device:TPU:1, one launch (start us, length us, event | category | flops | bytes accessed | tf_op | source)
XLA Modules:
  0.0 36.2 jit_solution(4059779630247436322)
XLA Ops:
  0.6 34.3 %basis.1 = (f32[17,192,128]{2,1,0:T(8,128)S(1)}, f32[9,192,128]{2,1,0:T(8,128)S(1)}, f32[1,128]{1,0:T(1,128)S(1)}) custom-call(s32[4096]{0:T(1024)} %fold_ref.1, f32[160,128]{1,0:T(8,128)} %forcing_ref.1, f32[160,128]{1,0:T(8,128)} %search_ref.1, f32[160,128]{1,0:T(8,128)} %depth_ref.1, s32[160,128]{1,0:T(8,128)} %mask_ref.1), custom_call_target="tpu_custom_call" | custom-call | tf_op jit(solution)/shard_map/basis/pallas_call | solution.py:578
  34.9 1.3 %combine.1 = (f32[160,128]{1,0:T(8,128)}, f32[160,128]{1,0:T(8,128)}) custom-call(f32[1,128]{1,0:T(1,128)S(1)} %get-tuple-element.5.moments_ref, f32[17,192,128]{2,1,0:T(8,128)S(1)} %get-tuple-element.6.basis_ref, f32[9,192,128]{2,1,0:T(8,128)S(1)} %get-tuple-element.7.strips_ref), custom_call_target="tpu_custom_call" | custom-call | tf_op jit(solution)/shard_map/combine/pallas_call | solution.py:696

commit v8 on v7

--- a/solution.py
+++ b/solution.py
@@ -384,12 +384,16 @@
             at = pl.ds(6 * n + c, 1)
             rows_acc[at, :] = rows_acc[at, :] + row
 
-    def steps(tasks):
+    def steps(tasks, unrolled):
         step(1, tasks, True, False)
-
-        @pl.loop(2, STEPS)
-        def _(n):
-            step(n, tasks, False, False)
+        if unrolled:
+            for n in range(2, STEPS):
+                step(n, tasks, False, False)
+        else:
+
+            @pl.loop(2, STEPS)
+            def _(n):
+                step(n, tasks, False, False)
 
         step(STEPS, tasks, False, True)
 
@@ -416,7 +420,7 @@
     def _():
         next_level(2)
 
-    steps(tasks("m", 16, 168, 32, 160))
+    steps(tasks("m", 16, 168, 32, 160), False)
 
     to_east.wait()
     to_west.wait()
@@ -433,7 +437,7 @@
 
     roots("s", [(17, 7)] + chunks(24, 168) + [(168, 7)])
     links("s", chunks(16, 168))
-    steps(tasks("s", 16, 168, 32, 160))
+    steps(tasks("s", 16, 168, 32, 160), True)
 
     @pl.when(jnp.logical_not(bottom))
     def _():
@@ -499,7 +503,7 @@
         fields(kind, [(LO, 8), (176, 8)])
         roots(kind, [(LO, 16), (168, 16)])
         links(kind, [(LO, 16), (168, 16)])
-    steps([(kind, r, 24, lo, lo + 16) for kind in ("m", "s") for r, lo in ((LO, 16), (160, 160))])
+    steps([(kind, r, 24, lo, lo + 16) for kind in ("m", "s") for r, lo in ((LO, 16), (160, 160))], True)
 
     ones = jnp.ones((8, COLS), F32)
     sums = lax.dot_general(

time: 36.3 us -> 37.9 us (1.044)
  Pallas kernels: 35.5 us -> 37.1 us
    pallas_call x1, Pallas kernels: 34.3 us -> 35.9 us  [basis_and_moments(): pl.pallas_call(basis_kernel, out_shape=(held((FIELDS,) + ext), held((STEP...]
where the time goes in v8:
time: 37.9 us; the launch traced here: 37.8 us
  Pallas kernels  37.1 us (98%)
  between operations  0.64 us (2%)
    pallas_call x1, Pallas kernels, basis_and_moments(): pl.pallas_call(basis_kernel, out_shape=(held((FIELDS,) + ext), held((STEP...  35.9 us
    pallas_call x1, Pallas kernels, per_device(): pl.pallas_call(combine_kernel, out_shape=(block, block), in_specs=[pl.Blo...  1.26 us

profile of v8, /device:TPU:1, one launch (start us, length us, event | category | flops | bytes accessed | tf_op | source)
XLA Modules:
  0.0 37.8 jit_solution(3652818536885290315)
XLA Ops:
  0.6 35.9 %basis.1 = (f32[17,192,128]{2,1,0:T(8,128)S(1)}, f32[9,192,128]{2,1,0:T(8,128)S(1)}, f32[1,128]{1,0:T(1,128)S(1)}) custom-call(s32[4096]{0:T(1024)} %fold_ref.1, f32[160,128]{1,0:T(8,128)} %forcing_ref.1, f32[160,128]{1,0:T(8,128)} %search_ref.1, f32[160,128]{1,0:T(8,128)} %depth_ref.1, s32[160,128]{1,0:T(8,128)} %mask_ref.1), custom_call_target="tpu_custom_call" | custom-call | tf_op jit(solution)/shard_map/basis/pallas_call | solution.py:582
  36.5 1.3 %combine.1 = (f32[160,128]{1,0:T(8,128)}, f32[160,128]{1,0:T(8,128)}) custom-call(f32[1,128]{1,0:T(1,128)S(1)} %get-tuple-element.5.moments_ref, f32[17,192,128]{2,1,0:T(8,128)S(1)} %get-tuple-element.6.basis_ref, f32[9,192,128]{2,1,0:T(8,128)S(1)} %get-tuple-element.7.strips_ref), custom_call_target="tpu_custom_call" | custom-call | tf_op jit(solution)/shard_map/combine/pallas_call | solution.py:700

commit v9 on v7

--- a/solution.py
+++ b/solution.py
@@ -15,6 +15,7 @@
 LO = 8
 FIELDS = 2 * STEPS + 1
 FIRST = STEPS + 1
+HALF = FIELDS + 1
 HIGHEST = lax.Precision.HIGHEST
 F32 = jnp.float32
 
@@ -130,6 +131,8 @@
             greet(plane_sem.at[level], around(1 << level))
 
     rows_acc[...] = jnp.zeros_like(rows_acc)
+    b_m[HALF + 2] = jnp.zeros((EXT, COLS), F32)
+    b_s[STEPS + 2] = jnp.zeros((EXT, COLS), F32)
     for copy in loads:
         copy.wait()
     raw_m[0, 16 : 16 + ROWS, :] = depth_buf[...] * mask_buf[...].astype(F32)
@@ -273,10 +276,14 @@
         for r, n in spans:
             wet = (kinds[kind][0][r : r + n, :] > 0.0).astype(F32)
             if kind == "m":
-                b_m[0, r : r + n, :] = wet * raw_m[2, r : r + n, :]
-                b_m[FIRST, r : r + n, :] = wet * raw_m[1, r : r + n, :]
+                for slot, half, source in ((0, HALF, 2), (FIRST, HALF + 1, 1)):
+                    value = wet * raw_m[source, r : r + n, :]
+                    b_m[slot, r : r + n, :] = value
+                    b_m[half, r : r + n, :] = 0.5 * value
             else:
-                b_s[0, r : r + n, :] = wet * side_state[r : r + n, :]
+                value = wet * side_state[r : r + n, :]
+                b_s[0, r : r + n, :] = value
+                b_s[STEPS + 1, r : r + n, :] = 0.5 * value
 
     def roots(kind, spans):
         depth_ref_, s, de, se, _ = kinds[kind]
@@ -328,7 +335,8 @@
         west_part = from_west(f_u * up + f_c * mid + f_d * low)
         return mid, (a_u * up + a_d * low) + (east_part + west_part)
 
-    def step(n, tasks, first, last):
+    def step(n, tasks):
+        first = n == 1
         total = {}
 
         def add(key, product, lo, hi):
@@ -342,11 +350,14 @@
                 w[4, r : r + size, :], w[2, r : r + size, :], w[5, r - 1 : r - 1 + size, :],
                 w[6, r : r + size, :], w[1, r : r + size, :], w[3, r - 1 : r - 1 + size, :],
             )
-            b, bases = (b_s, (0,)) if kind == "s" else (b_m, (0,) if last else (0, FIRST))
+            if kind == "s":
+                b, starts, zero = b_s, ((0, STEPS + 1),), STEPS + 2
+            else:
+                b, starts, zero = b_m, ((0, HALF), (FIRST, HALF + 1)), HALF + 2
             news, olds = [], []
-            for base in bases:
-                mid, out = apply(b, base + n - 1, weights, r, size)
-                out = 0.5 * out if first else out - b[base + n - 2, r : r + size, :]
+            for base, half in starts:
+                mid, out = apply(b, jnp.where(first, half, base + n - 1), weights, r, size)
+                out = out - b[jnp.where(first, zero, base + n - 2), r : r + size, :]
                 b[base + n, r : r + size, :] = out
                 news.append(out)
                 olds.append(mid)
@@ -360,19 +371,12 @@
                 add("s4", p1 * shift(p1, 64), lo, hi)
                 add("s5", p1 * shift(p0, 64), lo, hi)
                 continue
-            add("m0", p1 * p1, lo, hi)
-            add("m1", p1 * p0, lo, hi)
-            if last:
-                r0 = b_m[FIRST + STEPS - 1, r : r + size, :]
-            else:
-                r1, r0 = news[1], olds[1]
-                add("m2", r1 * r1, lo, hi)
-                add("m3", r1 * r0, lo, hi)
-                add("m4", p1 * r1, lo, hi)
-            add("m5", p1 * r0, lo, hi)
-        gather(n, total)
-
-    def gather(n, total):
+            r1, r0 = news[1], olds[1]
+            for c, product in enumerate((p1 * p1, p1 * p0, r1 * r1, r1 * r0, p1 * r1, p1 * r0)):
+                add("m%d" % c, product, lo, hi)
+        gather(n, total, jnp.where(first, 2.0, 1.0))
+
+    def gather(n, total, scale):
         rows = {key: jnp.sum(value, axis=0, keepdims=True) for key, value in total.items()}
         for c in range(6):
             row = jnp.zeros((1, COLS), F32)
@@ -381,17 +385,15 @@
             source = "s%d" % (c - 2 if c in (2, 3) else c)
             if source in rows:
                 row = row + jnp.where(strips_r if c in (2, 3) else strips_p, rows[source], 0.0)
+            if c % 2:
+                row = row * scale
             at = pl.ds(6 * n + c, 1)
             rows_acc[at, :] = rows_acc[at, :] + row
 
     def steps(tasks):
-        step(1, tasks, True, False)
-
-        @pl.loop(2, STEPS)
+        @pl.loop(1, STEPS + 1)
         def _(n):
-            step(n, tasks, False, False)
-
-        step(STEPS, tasks, False, True)
+            step(n, tasks)
 
     def tasks(kind, start, stop, gram_lo, gram_hi):
         return [(kind, r, n, gram_lo, gram_hi) for r, n in chunks(start, stop)]
@@ -410,7 +412,7 @@
         p0, r0 = b_m[0, r : r + n, :], b_m[FIRST, r : r + n, :]
         for key, value in (("m0", p0 * p0), ("m2", r0 * r0), ("m4", p0 * r0)):
             start[key] = start[key] + fold8(value) if key in start else fold8(value)
-    gather(0, start)
+    gather(0, start, 1.0)
 
     @pl.when(jnp.logical_not(top))
     def _():
@@ -429,7 +431,7 @@
         p0 = b_s[0, r : r + n, :]
         for key, value in (("s0", p0 * p0), ("s4", p0 * shift(p0, 64))):
             start[key] = start[key] + fold8(value) if key in start else fold8(value)
-    gather(0, start)
+    gather(0, start, 1.0)
 
     roots("s", [(17, 7)] + chunks(24, 168) + [(168, 7)])
     links("s", chunks(16, 168))
@@ -577,7 +579,7 @@
     ext = (EXT, COLS)
     return pl.pallas_call(
         basis_kernel,
-        out_shape=(held((FIELDS,) + ext), held((STEPS + 1,) + ext), held((1, COLS))),
+        out_shape=(held((HALF + 3,) + ext), held((STEPS + 3,) + ext), held((1, COLS))),
         in_specs=[pl.BlockSpec(memory_space=pl.ANY)] * 5,
         out_specs=(pl.BlockSpec(memory_space=vm),) * 3,
         scratch_shapes=[

time: 36.3 us -> 53.9 us (1.48)
  Pallas kernels: 35.5 us -> 53.1 us
    pallas_call x1, Pallas kernels: 34.3 us -> 51.8 us  [basis_and_moments(): pl.pallas_call(basis_kernel, out_shape=(held((HALF + 3,) + ext), held((ST...]
where the time goes in v9:
time: 53.9 us; the launch traced here: 53.7 us
  Pallas kernels  53.1 us (99%)
  between operations  0.64 us (1%)
    pallas_call x1, Pallas kernels, basis_and_moments(): pl.pallas_call(basis_kernel, out_shape=(held((HALF + 3,) + ext), held((ST...  51.8 us
    pallas_call x1, Pallas kernels, per_device(): pl.pallas_call(combine_kernel, out_shape=(block, block), in_specs=[pl.Blo...  1.26 us

profile of v9, /device:TPU:1, one launch (start us, length us, event | category | flops | bytes accessed | tf_op | source)
XLA Modules:
  0.0 53.7 jit_solution(13935511331039063788)
XLA Ops:
  0.6 51.8 %basis.1 = (f32[21,192,128]{2,1,0:T(8,128)S(1)}, f32[11,192,128]{2,1,0:T(8,128)S(1)}, f32[1,128]{1,0:T(1,128)S(1)}) custom-call(s32[4096]{0:T(1024)} %fold_ref.1, f32[160,128]{1,0:T(8,128)} %forcing_ref.1, f32[160,128]{1,0:T(8,128)} %search_ref.1, f32[160,128]{1,0:T(8,128)} %depth_ref.1, s32[160,128]{1,0:T(8,128)} %mask_ref.1), custom_call_target="tpu_custom_call" | custom-call | tf_op jit(solution)/shard_map/basis/pallas_call | solution.py:580
  52.5 1.3 %combine.1 = (f32[160,128]{1,0:T(8,128)}, f32[160,128]{1,0:T(8,128)}) custom-call(f32[1,128]{1,0:T(1,128)S(1)} %get-tuple-element.5.moments_ref, f32[21,192,128]{2,1,0:T(8,128)S(1)} %get-tuple-element.6.basis_ref, f32[11,192,128]{2,1,0:T(8,128)S(1)} %get-tuple-element.7.strips_ref), custom_call_target="tpu_custom_call" | custom-call | tf_op jit(solution)/shard_map/combine/pallas_call | solution.py:698

commit v10 on v7

--- a/solution.py
+++ b/solution.py
@@ -328,7 +328,7 @@
         west_part = from_west(f_u * up + f_c * mid + f_d * low)
         return mid, (a_u * up + a_d * low) + (east_part + west_part)
 
-    def step(n, tasks, first, last):
+    def step(n, tasks, first):
         total = {}
 
         def add(key, product, lo, hi):
@@ -342,7 +342,7 @@
                 w[4, r : r + size, :], w[2, r : r + size, :], w[5, r - 1 : r - 1 + size, :],
                 w[6, r : r + size, :], w[1, r : r + size, :], w[3, r - 1 : r - 1 + size, :],
             )
-            b, bases = (b_s, (0,)) if kind == "s" else (b_m, (0,) if last else (0, FIRST))
+            b, bases = (b_s, (0,)) if kind == "s" else (b_m, (0, FIRST))
             news, olds = [], []
             for base in bases:
                 mid, out = apply(b, base + n - 1, weights, r, size)
@@ -360,16 +360,9 @@
                 add("s4", p1 * shift(p1, 64), lo, hi)
                 add("s5", p1 * shift(p0, 64), lo, hi)
                 continue
-            add("m0", p1 * p1, lo, hi)
-            add("m1", p1 * p0, lo, hi)
-            if last:
-                r0 = b_m[FIRST + STEPS - 1, r : r + size, :]
-            else:
-                r1, r0 = news[1], olds[1]
-                add("m2", r1 * r1, lo, hi)
-                add("m3", r1 * r0, lo, hi)
-                add("m4", p1 * r1, lo, hi)
-            add("m5", p1 * r0, lo, hi)
+            r1, r0 = news[1], olds[1]
+            for c, product in enumerate((p1 * p1, p1 * p0, r1 * r1, r1 * r0, p1 * r1, p1 * r0)):
+                add("m%d" % c, product, lo, hi)
         gather(n, total)
 
     def gather(n, total):
@@ -385,13 +378,11 @@
             rows_acc[at, :] = rows_acc[at, :] + row
 
     def steps(tasks):
-        step(1, tasks, True, False)
-
-        @pl.loop(2, STEPS)
+        step(1, tasks, True)
+
+        @pl.loop(2, STEPS + 1)
         def _(n):
-            step(n, tasks, False, False)
-
-        step(STEPS, tasks, False, True)
+            step(n, tasks, False)
 
     def tasks(kind, start, stop, gram_lo, gram_hi):
         return [(kind, r, n, gram_lo, gram_hi) for r, n in chunks(start, stop)]
@@ -577,7 +568,7 @@
     ext = (EXT, COLS)
     return pl.pallas_call(
         basis_kernel,
-        out_shape=(held((FIELDS,) + ext), held((STEPS + 1,) + ext), held((1, COLS))),
+        out_shape=(held((FIELDS + 1,) + ext), held((STEPS + 1,) + ext), held((1, COLS))),
         in_specs=[pl.BlockSpec(memory_space=pl.ANY)] * 5,
         out_specs=(pl.BlockSpec(memory_space=vm),) * 3,
         scratch_shapes=[

time: 36.3 us -> 36.4 us (level)
  no operation moved by 1% of the time
where the time goes in v10:
time: 36.4 us; the launch traced here: 36.2 us
  Pallas kernels  35.6 us (98%)
  between operations  0.64 us (2%)
    pallas_call x1, Pallas kernels, basis_and_moments(): pl.pallas_call(basis_kernel, out_shape=(held((FIELDS + 1,) + ext), held((...  34.3 us
    pallas_call x1, Pallas kernels, per_device(): pl.pallas_call(combine_kernel, out_shape=(block, block), in_specs=[pl.Blo...  1.26 us

profile of v10, /device:TPU:1, one launch (start us, length us, event | category | flops | bytes accessed | tf_op | source)
XLA Modules:
  0.0 36.2 jit_solution(13513412762759247583)
XLA Ops:
  0.6 34.3 %basis.1 = (f32[18,192,128]{2,1,0:T(8,128)S(1)}, f32[9,192,128]{2,1,0:T(8,128)S(1)}, f32[1,128]{1,0:T(1,128)S(1)}) custom-call(s32[4096]{0:T(1024)} %fold_ref.1, f32[160,128]{1,0:T(8,128)} %forcing_ref.1, f32[160,128]{1,0:T(8,128)} %search_ref.1, f32[160,128]{1,0:T(8,128)} %depth_ref.1, s32[160,128]{1,0:T(8,128)} %mask_ref.1), custom_call_target="tpu_custom_call" | custom-call | tf_op jit(solution)/shard_map/basis/pallas_call | solution.py:569
  35.0 1.3 %combine.1 = (f32[160,128]{1,0:T(8,128)}, f32[160,128]{1,0:T(8,128)}) custom-call(f32[1,128]{1,0:T(1,128)S(1)} %get-tuple-element.5.moments_ref, f32[18,192,128]{2,1,0:T(8,128)S(1)} %get-tuple-element.6.basis_ref, f32[9,192,128]{2,1,0:T(8,128)S(1)} %get-tuple-element.7.strips_ref), custom_call_target="tpu_custom_call" | custom-call | tf_op jit(solution)/shard_map/combine/pallas_call | solution.py:687

commit v11 on v10

--- a/solution.py
+++ b/solution.py
@@ -15,6 +15,7 @@
 LO = 8
 FIELDS = 2 * STEPS + 1
 FIRST = STEPS + 1
+OTHER = STEPS + 2
 HIGHEST = lax.Precision.HIGHEST
 F32 = jnp.float32
 
@@ -130,6 +131,8 @@
             greet(plane_sem.at[level], around(1 << level))
 
     rows_acc[...] = jnp.zeros_like(rows_acc)
+    for ref, slot in ((b_m, 0), (b_m, OTHER), (b_s, 0)):
+        ref[slot] = jnp.zeros((EXT, COLS), F32)
     for copy in loads:
         copy.wait()
     raw_m[0, 16 : 16 + ROWS, :] = depth_buf[...] * mask_buf[...].astype(F32)
@@ -273,10 +276,10 @@
         for r, n in spans:
             wet = (kinds[kind][0][r : r + n, :] > 0.0).astype(F32)
             if kind == "m":
-                b_m[0, r : r + n, :] = wet * raw_m[2, r : r + n, :]
-                b_m[FIRST, r : r + n, :] = wet * raw_m[1, r : r + n, :]
+                b_m[1, r : r + n, :] = wet * raw_m[2, r : r + n, :]
+                b_m[OTHER + 1, r : r + n, :] = wet * raw_m[1, r : r + n, :]
             else:
-                b_s[0, r : r + n, :] = wet * side_state[r : r + n, :]
+                b_s[1, r : r + n, :] = wet * side_state[r : r + n, :]
 
     def roots(kind, spans):
         depth_ref_, s, de, se, _ = kinds[kind]
@@ -328,7 +331,8 @@
         west_part = from_west(f_u * up + f_c * mid + f_d * low)
         return mid, (a_u * up + a_d * low) + (east_part + west_part)
 
-    def step(n, tasks, first):
+    def step(n, tasks):
+        scale = jnp.where(n == 1, 0.5, 1.0)
         total = {}
 
         def add(key, product, lo, hi):
@@ -342,12 +346,12 @@
                 w[4, r : r + size, :], w[2, r : r + size, :], w[5, r - 1 : r - 1 + size, :],
                 w[6, r : r + size, :], w[1, r : r + size, :], w[3, r - 1 : r - 1 + size, :],
             )
-            b, bases = (b_s, (0,)) if kind == "s" else (b_m, (0, FIRST))
+            b, bases = (b_s, (0,)) if kind == "s" else (b_m, (0, OTHER))
             news, olds = [], []
             for base in bases:
-                mid, out = apply(b, base + n - 1, weights, r, size)
-                out = 0.5 * out if first else out - b[base + n - 2, r : r + size, :]
-                b[base + n, r : r + size, :] = out
+                mid, out = apply(b, base + n, weights, r, size)
+                out = scale * out - b[base + n - 1, r : r + size, :]
+                b[base + n + 1, r : r + size, :] = out
                 news.append(out)
                 olds.append(mid)
             lo, hi = max(r, gram_lo) - r, min(r + size, gram_hi) - r
@@ -378,11 +382,9 @@
             rows_acc[at, :] = rows_acc[at, :] + row
 
     def steps(tasks):
-        step(1, tasks, True)
-
-        @pl.loop(2, STEPS + 1)
+        @pl.loop(1, STEPS + 1)
         def _(n):
-            step(n, tasks, False)
+            step(n, tasks)
 
     def tasks(kind, start, stop, gram_lo, gram_hi):
         return [(kind, r, n, gram_lo, gram_hi) for r, n in chunks(start, stop)]
@@ -398,7 +400,7 @@
 
     start = {}
     for r, n in chunks(16, 176):
-        p0, r0 = b_m[0, r : r + n, :], b_m[FIRST, r : r + n, :]
+        p0, r0 = b_m[1, r : r + n, :], b_m[OTHER + 1, r : r + n, :]
         for key, value in (("m0", p0 * p0), ("m2", r0 * r0), ("m4", p0 * r0)):
             start[key] = start[key] + fold8(value) if key in start else fold8(value)
     gather(0, start)
@@ -417,7 +419,7 @@
     fields("s", chunks(16, 176))
     start = {}
     for r, n in chunks(16, 176):
-        p0 = b_s[0, r : r + n, :]
+        p0 = b_s[1, r : r + n, :]
         for key, value in (("s0", p0 * p0), ("s4", p0 * shift(p0, 64))):
             start[key] = start[key] + fold8(value) if key in start else fold8(value)
     gather(0, start)
@@ -568,7 +570,7 @@
     ext = (EXT, COLS)
     return pl.pallas_call(
         basis_kernel,
-        out_shape=(held((FIELDS + 1,) + ext), held((STEPS + 1,) + ext), held((1, COLS))),
+        out_shape=(held((2 * OTHER,) + ext), held((OTHER,) + ext), held((1, COLS))),
         in_specs=[pl.BlockSpec(memory_space=pl.ANY)] * 5,
         out_specs=(pl.BlockSpec(memory_space=vm),) * 3,
         scratch_shapes=[
@@ -672,8 +674,8 @@
             mixed.append(jnp.where(search_half, coords[n], other))
         for at in range(0, ROWS, size):
             rows = slice(16 + at, 16 + at + size)
-            main = sum(coords[k] * basis_ref[k, rows, :] for k in range(FIELDS))
-            strip = sum(mixed[n] * strips_ref[n, rows, :] for n in range(STEPS + 1))
+            main = sum(coords[k] * basis_ref[k + 1 if k < FIRST else OTHER + 1 + k - FIRST, rows, :] for k in range(FIELDS))
+            strip = sum(mixed[n] * strips_ref[n + 1, rows, :] for n in range(STEPS + 1))
             strip = strip + shift(strip, 64)
             out_ref[at : at + size, :] = jnp.where(
                 lane1 >= 119, strip, jnp.where(lane1 < 9, shift(strip, -WEST), main)

time: 36.4 us -> 36.5 us (level)
  no operation moved by 1% of the time
where the time goes in v11:
time: 36.5 us; the launch traced here: 36.4 us
  Pallas kernels  35.7 us (98%)
  between operations  0.64 us (2%)
    pallas_call x1, Pallas kernels, basis_and_moments(): pl.pallas_call(basis_kernel, out_shape=(held((2 * OTHER,) + ext), held((O...  34.4 us
    pallas_call x1, Pallas kernels, per_device(): pl.pallas_call(combine_kernel, out_shape=(block, block), in_specs=[pl.Blo...  1.26 us

profile of v11, /device:TPU:1, one launch (start us, length us, event | category | flops | bytes accessed | tf_op | source)
XLA Modules:
  0.0 36.4 jit_solution(10981872742601473093)
XLA Ops:
  0.6 34.4 %basis.1 = (f32[20,192,128]{2,1,0:T(8,128)S(1)}, f32[10,192,128]{2,1,0:T(8,128)S(1)}, f32[1,128]{1,0:T(1,128)S(1)}) custom-call(s32[4096]{0:T(1024)} %fold_ref.1, f32[160,128]{1,0:T(8,128)} %forcing_ref.1, f32[160,128]{1,0:T(8,128)} %search_ref.1, f32[160,128]{1,0:T(8,128)} %depth_ref.1, s32[160,128]{1,0:T(8,128)} %mask_ref.1), custom_call_target="tpu_custom_call" | custom-call | tf_op jit(solution)/shard_map/basis/pallas_call | solution.py:571
  35.1 1.3 %combine.1 = (f32[160,128]{1,0:T(8,128)}, f32[160,128]{1,0:T(8,128)}) custom-call(f32[1,128]{1,0:T(1,128)S(1)} %get-tuple-element.5.moments_ref, f32[20,192,128]{2,1,0:T(8,128)S(1)} %get-tuple-element.6.basis_ref, f32[10,192,128]{2,1,0:T(8,128)S(1)} %get-tuple-element.7.strips_ref), custom_call_target="tpu_custom_call" | custom-call | tf_op jit(solution)/shard_map/combine/pallas_call | solution.py:689
